TPU v7x, 256 devices: a whole 4x4x8 slice. The times are simulated.
256 devices in a mesh: section: 8 (over z), dp: 32 (over x, y, core).
Axes of the slice: x: 4, y: 4, z: 8, core: 2. Of those that a mesh axis runs over, the one named last changes fastest.
Arguments:
- inject: bfloat16 [8, 256, 4096], P('section', 'dp'), may hold values from -42 to 42, as said below
- w_gate: bfloat16 [8, 4096, 11008], P('section', None, 'dp'), may hold values from -0.09375 to 0.09375
- w_up: bfloat16 [8, 4096, 11008], P('section', None, 'dp'), may hold values from -0.09375 to 0.09375
- w_down: bfloat16 [8, 11008, 4096], P('section', 'dp'), may hold values from -0.0546875 to 0.0546875
- gain: float32 [8, 4096], P('section'), may hold values from 0.5 to 1.5
Outputs:
- iterate: float32 [8, 256, 4096], P('section', 'dp')
- mixing: float32 [8, 5, 5], P('section')
Inputs may be any that keep to these rules, and one draw needn't show every extreme that they name: inject has entries of varied magnitude from token to token.
All inputs are finite; a program needn't handle non-finite values.
Results may differ from a plain program's by a relative error of at most 0.0038.
Values may be sent and summed in bfloat16 or wider, within the bound.
No kernel may reach another device: no remote copies, remote signals or barrier semaphores. Data moves between devices by JAX's collectives and lax.ppermute only.
A program may use at most 64 MiB of HBM per device.

v0:
```python
import functools

import jax
import jax.numpy as jnp
from jax import lax
from jax.experimental import pallas as pl
from jax.experimental.pallas import tpu as pltpu
from jax.sharding import PartitionSpec as P

ITERS = 5
HIST = 5
F32 = jnp.float32
BF16 = jnp.bfloat16
EXTRA = 256


MIB = 1024 * 1024
RING = tuple(
    4 * x + y
    for x, y in ((0, 0), (0, 1), (0, 2), (0, 3), (1, 3), (1, 2), (1, 1), (2, 1))
    + ((2, 2), (2, 3), (3, 3), (3, 2), (3, 1), (3, 0), (2, 0), (1, 0))
)


def pallas(body, out_shape, name, limit, scratch=()):
    return pl.pallas_call(
        body,
        out_shape=out_shape,
        scratch_shapes=list(scratch),
        name=name,
        compiler_params=pltpu.CompilerParams(vmem_limit_bytes=limit * MIB),
    )


def silu_times(gate, up):
    return gate / (1.0 + jnp.exp(-gate)) * up


def normalized(values, gain):
    mean = jnp.mean(values * values, axis=-1, keepdims=True)
    return (values * lax.rsqrt(mean + 1e-06) * gain).astype(BF16)


def by_rows(a, b):
    return lax.dot_general(a, b, (((1,), (1,)), ((), ())), preferred_element_type=F32)


def start_body(gain_ref, gate_ref, up_ref, down_ref, part_ref):
    features = gate_ref.shape[1]
    normed = normalized(jnp.zeros((8, features), F32), gain_ref[...])
    gate = by_rows(normed, gate_ref[...])
    up = by_rows(normed, up_ref[...])
    act = silu_times(gate, up).astype(BF16)
    piece = features // 8
    row = lax.broadcasted_iota(jnp.int32, (8, piece), 0)
    folded = jnp.zeros((8, piece), F32)
    for r in range(8):
        out = jnp.dot(act, down_ref[:, r * piece : (r + 1) * piece], preferred_element_type=F32)
        folded = folded + jnp.where(row == r, out, 0.0)
    part_ref[...] = folded.astype(BF16)


def entry(row, lane):
    return row[:, lane : lane + 1]


def solved_weights(entries, iteration):
    count = iteration + 1
    trace = entries[0][0]
    for i in range(1, count):
        trace = trace + entries[i][i]
    damp = 0.01 * trace / count + 1e-06
    rows = [[entries[i][j] for j in range(count)] for i in range(count)]
    for i in range(count):
        rows[i][i] = rows[i][i] + damp
    values = [jnp.ones((1, 1), F32) for _ in range(count)]
    for p in range(count):
        for i in range(p + 1, count):
            factor = rows[i][p] / rows[p][p]
            for j in range(p, count):
                rows[i][j] = rows[i][j] - factor * rows[p][j]
            values[i] = values[i] - factor * values[p]
    beta = [None] * count
    for i in range(count - 1, -1, -1):
        accum = values[i]
        for j in range(i + 1, count):
            accum = accum - rows[i][j] * beta[j]
        beta[i] = accum / rows[i][i]
    total = beta[0]
    for i in range(1, count):
        total = total + beta[i]
    return [b / total for b in beta]


def lane_row(values):
    lane = lax.broadcasted_iota(jnp.int32, (1, 128), 1)
    out = jnp.zeros((1, 128), F32)
    for j, value in enumerate(values):
        out = out + jnp.where(lane == j, value, 0.0)
    return out


def gram_and_weights(extras, state, iteration, cells):
    chips = extras.shape[0] // 8
    sums = extras[0:8].astype(F32)
    for h in range(1, chips):
        sums = sums + extras[8 * h : 8 * h + 8].astype(F32)
    sums = sums[:, :128] + sums[:, 128:]
    fresh = (sums[2:3] + sums[1:2] + sums[0:1]) / cells
    known = [fresh] if state is None else [state[i : i + 1] for i in range(iteration)] + [fresh]
    if state is None:
        known = [lane_row([entry(fresh, 8)]), fresh]
    entries = [[None] * (iteration + 1) for _ in range(iteration + 1)]
    for i in range(iteration + 1):
        for j in range(i + 1):
            entries[i][j] = entries[j][i] = entry(known[i], j)
    weights = solved_weights(entries, iteration)
    kept = known + [jnp.zeros((8 - len(known), 128), F32)]
    return jnp.concatenate(kept, axis=0), weights, entries


def weight_rows(weights, entries, first):
    rows = [lane_row(weights)]
    if first:
        rows.append(lane_row(solved_weights(entries, 0)))
    rows.append(jnp.zeros((8 - len(rows), 128), F32))
    return jnp.concatenate(rows, axis=0)


def start_row(first_ref, features):
    tokens = first_ref.shape[0]
    sums = first_ref[0:8, features:].astype(F32)
    for h in range(1, tokens // 8):
        sums = sums + first_ref[8 * h : 8 * h + 8, features:].astype(F32)
    sums = sums.astype(BF16).astype(F32)
    return jnp.concatenate([sums[r : r + 1] for r in range(8)], axis=1)


def send_block(normed_ref, weights, part_ref):
    acts = []
    for gate_ref, up_ref in (weights[0:2], weights[3:5]):
        gate = by_rows(gate_ref[...], normed_ref[...])
        up = by_rows(up_ref[...], normed_ref[...])
        acts.append(jnp.transpose(silu_times(gate, up)).astype(BF16))
    features = part_ref.shape[1]
    step = min(512, features)
    for n in range(0, features, step):
        cols = slice(n, n + step)
        part = jnp.dot(acts[0], weights[2][:, cols], preferred_element_type=F32)
        part = part + jnp.dot(acts[1], weights[5][:, cols], preferred_element_type=F32)
        part_ref[:, cols] = part.astype(BF16)


def first_block_body(first_ref, own_ref, gain_ref, *refs):
    weights, (part_ref, image_ref, normed_ref) = refs[:6], refs[6:]
    tokens, features = part_ref.shape
    half = 0.5 * start_row(first_ref, features)
    image_ref[...] = own_ref[...].astype(F32) + half
    for h in range(0, tokens, 16):
        rows = first_ref[h : h + 16, :features].astype(F32) + half
        normed_ref[h : h + 16, :] = normalized(rows, gain_ref[...])
    send_block(normed_ref, weights, part_ref)


def block_body(iteration, cells, *refs):
    live = iteration
    first_ref = refs[0]
    outs = refs[1:live]
    images = refs[live : 2 * live]
    at = 2 * live
    state_ref = None
    if iteration > 2:
        state_ref = refs[at]
        at += 1
    gain_ref = refs[at]
    weights = refs[at + 1 : at + 7]
    part_ref, x_ref, kept_ref, mix_ref, normed_ref = refs[at + 7 :]
    tokens, features = part_ref.shape
    state = None if state_ref is None else state_ref[...]
    kept, mix, entries = gram_and_weights(outs[-1][:, features:], state, iteration - 1, cells)
    kept_ref[...] = kept
    mix_ref[...] = weight_rows(mix, entries, iteration == 2)
    x = mix[0] * images[0][...]
    for i in range(1, live):
        x = x + mix[i] * images[i][...]
    x_ref[...] = x
    total = mix[0]
    for i in range(1, live):
        total = total + mix[i]
    base = (0.5 * mix[0]) * start_row(first_ref, features)
    for h in range(0, tokens, 16):
        rows = total * first_ref[h : h + 16, :features].astype(F32) + base
        for i in range(1, live):
            rows = rows + (0.5 * mix[i]) * outs[i - 1][h : h + 16, :features].astype(F32)
        normed_ref[h : h + 16, :] = normalized(rows, gain_ref[...])
    send_block(normed_ref, weights, part_ref)


def split_in_three(values):
    high = values.astype(BF16).astype(F32)
    rest = values - high
    mid = rest.astype(BF16).astype(F32)
    low = rest - mid
    return [high, mid, low]


def inner(a, b):
    return jnp.sum(jnp.sum(a * b, axis=0, keepdims=True), axis=1, keepdims=True)


def image_body(iteration, before_ref, inject_ref, x_ref, *refs):
    misfits = refs[:iteration]
    image_ref, misfit_ref, extra_ref = refs[iteration:]
    image = inject_ref[...].astype(F32) + 0.5 * before_ref[...].astype(F32)
    misfit = image - x_ref[...]
    image_ref[...] = image
    misfit_ref[...] = misfit
    values = [inner(misfit, misfits[j][...]) for j in range(iteration)] + [inner(misfit, misfit)]
    row = lane_row(values)
    if iteration == 1:
        lane = lax.broadcasted_iota(jnp.int32, (1, 128), 1)
        first = misfits[0][...]
        row = row + jnp.where(lane == 8, inner(first, first), 0.0)
    pieces = split_in_three(row)
    extra_ref[...] = jnp.concatenate(pieces + [jnp.zeros((5, 128), F32)], axis=0).astype(BF16)


def final_body(cells, *refs):
    extra_ref = refs[0]
    images = refs[1 : 1 + HIST]
    state_ref = refs[1 + HIST]
    x_ref, mix_ref = refs[2 + HIST :]
    _, mix, entries = gram_and_weights(extra_ref[...], state_ref[...], ITERS - 1, cells)
    mix_ref[...] = weight_rows(mix, entries, False)
    x = mix[0] * images[0][...]
    for i in range(1, HIST):
        x = x + mix[i] * images[i][...]
    x_ref[...] = x


def local(inject, w_gate, w_up, w_down, gain):
    rows, features = inject.shape[1:]
    sections = lax.axis_size("section")
    groups = lax.axis_size("dp")
    chips = groups // 2
    tokens = rows * chips
    cells = float(rows * groups * features)
    hidden = w_gate.shape[2]
    order = RING if chips == len(RING) else tuple(range(chips))
    same_core = [[2 * h + c for h in order] for c in range(2)]
    across = [(d, d ^ 1) for d in range(groups)]
    ahead = [(s, (s + 1) % sections) for s in range(sections)]
    ahead_across = [
        (s * groups + d, (s + 1) % sections * groups + (d ^ 1))
        for s in range(sections)
        for d in range(groups)
    ]
    both = ("section", "dp")

    def to_chips(array):
        return lax.all_to_all(array, "dp", 0, 0, tiled=True, axis_index_groups=same_core)

    def to_all(block):
        wider = jnp.broadcast_to(block[None], (chips, *block.shape))
        return to_chips(wider).reshape(chips * block.shape[0], block.shape[1])

    shape = jax.ShapeDtypeStruct
    mine = inject[0]
    mine_w = [w_gate[0].T, w_up[0].T, w_down[0]]
    other_w = [lax.ppermute(w, "dp", across) for w in mine_w]
    part0 = pallas(start_body, shape((8, features // 8), BF16), "start", 12)(gain, *mine_w)
    near = lax.ppermute(part0, "section", ahead)
    far = lax.ppermute(part0, both, ahead_across)
    start_part = (near.astype(F32) + far.astype(F32)).astype(BF16)
    first = to_all(jnp.concatenate([mine, start_part], axis=1))

    part_shape = shape((tokens, features), BF16)
    own_shape = shape((rows, features), F32)
    small = shape((8, 128), F32)
    scratch = [pltpu.VMEM((tokens, features), BF16)]
    weights = mine_w + other_w
    images, misfits, gathered, mixing = [], [], [], []
    state = None
    for iteration in range(1, ITERS):
        if iteration == 1:
            part, x = pallas(first_block_body, (part_shape, own_shape), "block1", 12, scratch)(
                first, mine, gain, *weights
            )
            images.append(x)
            misfits.append(x)
        else:
            body = functools.partial(block_body, iteration, cells)
            carried = [] if state is None else [state]
            arrays = (first, *gathered, *images, *carried, gain, *weights)
            part, x, state, mix = pallas(
                body, (part_shape, own_shape, small, small), f"block{iteration}", 12, scratch
            )(first, *gathered, *images, *carried, gain, *weights)
            if iteration == 2:
                mixing.append(mix[1, :HIST])
            mixing.append(mix[0, :HIST])
        summed = jnp.sum(to_chips(part.reshape(chips, rows, features)).astype(F32), axis=0)
        before = lax.ppermute((x + summed).astype(BF16), "section", ahead)
        image, misfit, extra = pallas(
            functools.partial(image_body, iteration),
            (own_shape, own_shape, shape((8, 128), BF16)),
            f"image{iteration}",
            8,
        )(before, mine, x, *misfits)
        images.append(image)
        misfits.append(misfit)
        payload = [extra, lax.ppermute(extra, "dp", across)]
        if iteration < ITERS - 1:
            payload = [before] + payload
        gathered.append(to_all(jnp.concatenate(payload, axis=1)))
    iterate, mix = pallas(
        functools.partial(final_body, cells), (shape((rows, features), F32), small), "final", 8
    )(gathered[-1], *images, state)
    mixing.append(mix[0, :HIST])
    return iterate[None], jnp.stack(mixing)[None]


def solution(mesh):
    placed = (
        P("section", "dp", None),
        P("section", None, "dp"),
        P("section", None, "dp"),
        P("section", "dp", None),
        P("section", None),
    )
    return jax.shard_map(
        local,
        mesh=mesh,
        in_specs=placed,
        out_specs=(P("section", "dp", None), P("section", None, None)),
        check_vma=False,
    )
```

profile of v0, /device:TPU:1, one launch (start us, length us, event | category | flops | bytes accessed | tf_op | source)
XLA Modules:
  0.0 249.0 jit_solution(17941922919898094310)
XLA Ops:
  0.6 3.3 %collective-permute-start.2 = (bf16[344,4096]{1,0:T(8,128)(2,1)}, bf16[344,4096]{1,0:T(8,128)(2,1)S(1)}, u32[]{:S(2)}, u32[]{:S(2)}) collective-permute-start(bf16[344,4096]{1,0:T(8,128)(2,1)} %bitcast.19), channel_id=1, source_target_pairs={{0,1},{1,0},{2,3},{3,2},{4,5},{5,4},{6,7},{7,6},{8,9},{9,8},{10,11... | collective-permute-start | bytes 8454152 | tf_op jit(solution)/shard_map/ppermute | solution.py:270
  3.9 0.1 collective-permute-start.3
  4.0 0.4 collective-permute-start.4
  4.4 1.8 copy-done
  6.2 1.8 copy-done.2
  8.0 1.8 copy-done.4
  9.8 0.7 copy-done.6
  10.5 2.1 start.1
  12.8 1.5 collective-permute-start
  14.3 3.7 %collective-permute-done.1 = bf16[8,512]{1,0:T(8,128)(2,1)S(1)} collective-permute-done((bf16[8,512]{1,0:T(8,128)(2,1)S(1)}, bf16[8,512]{1,0:T(8,128)(2,1)S(1)}, u32[]{:S(2)}, u32[]{:S(2)}) %collective-permute-start.1) | collective-permute-done | bytes 8224 | tf_op jit(solution)/shard_map/ppermute | solution.py:273
  18.1 23.9 %all_to_all.45 = bf16[16,8,4608]{2,1,0:T(8,128)(2,1)S(1)} all-to-all(bf16[16,8,4608]{2,1,0:T(8,128)(2,1)S(1)} %broadcast_in_dim.14), channel_id=1, replica_groups={{0,2,4,6,14,12,10,18,20,22,30,28,26,24,16,8},{1,3,5,7,15,13,11,19,21,23..., dimensions={0} | all-to-all | bytes 2359296 | tf_op jit(solution)/shard_map/all_to_all | solution.py:261
  42.0 4.8 %block1.1 = (bf16[128,4096]{1,0:T(8,128)(2,1)S(1)}, f32[8,4096]{1,0:T(8,128)S(1)}) custom-call(bf16[128,4608]{1,0:T(8,128)(2,1)S(1)} %bitcast.37, bf16[8,4096]{1,0:T(8,128)(2,1)S(1)} %bitcast.48, f32[1,4096]{1,0:T(1,128)S(1)} %copy-done.7, bf16[344,4096]{1,0:T(8,128)(2,1)S(1)} %bitcast.21, bf16[344,4096]{1,0:T(8,128)(2,1)S(1)} %bitcast.27, ...), custom_call_target="tpu_custom_call" | custom-call | tf_op jit(solution)/shard_map/block1/pallas_call | solution.py:286
  46.8 17.0 %all_to_all.46 = bf16[16,8,4096]{2,1,0:T(8,128)(2,1)S(1)} all-to-all(bf16[16,8,4096]{2,1,0:T(8,128)(2,1)S(1)} %bitcast.56), channel_id=1, replica_groups={{0,2,4,6,14,12,10,18,20,22,30,28,26,24,16,8},{1,3,5,7,15,13,11,19,21,23..., dimensions={0} | all-to-all | bytes 2097152 | tf_op jit(solution)/shard_map/all_to_all | solution.py:261
  63.8 0.1 convert_reduce_fusion.3
  64.1 4.3 %collective-permute-done.5.before_ref = bf16[8,4096]{1,0:T(8,128)(2,1)S(1)} collective-permute-done((bf16[8,4096]{1,0:T(8,128)(2,1)S(1)}, bf16[8,4096]{1,0:T(8,128)(2,1)S(1)}, u32[]{:S(2)}, u32[]{:S(2)}) %collective-permute-start.5) | collective-permute-done | bytes 65568 | tf_op jit(solution)/shard_map/ppermute | solution.py:302
  68.4 0.2 image1.1
  68.6 4.5 %collective-permute-start.6 = (bf16[8,128]{1,0:T(8,128)(2,1)S(1)}, bf16[8,128]{1,0:T(8,128)(2,1)S(1)}, u32[]{:S(2)}, u32[]{:S(2)}) collective-permute-start(bf16[8,128]{1,0:T(8,128)(2,1)S(1)} %get-tuple-element.31), channel_id=1, source_target_pairs={{0,1},{1,0},{2,3},{3,2},{4,5},{5,4},{6,7},{7,6},{8,9},{9,8},{10,11... | collective-permute-start | bytes 6152 | tf_op jit(solution)/shard_map/ppermute | solution.py:311
  73.1 0.8 collective-permute-done.6
  74.0 20.7 %all_to_all.47 = bf16[16,8,4352]{2,1,0:T(8,128)(2,1)S(1)} all-to-all(bf16[16,8,4352]{2,1,0:T(8,128)(2,1)S(1)} %broadcast_in_dim.15), channel_id=1, replica_groups={{0,2,4,6,14,12,10,18,20,22,30,28,26,24,16,8},{1,3,5,7,15,13,11,19,21,23..., dimensions={0} | all-to-all | bytes 2228224 | tf_op jit(solution)/shard_map/all_to_all | solution.py:261
  94.7 5.4 %block2.1 = (bf16[128,4096]{1,0:T(8,128)(2,1)S(1)}, f32[8,4096]{1,0:T(8,128)S(1)}, f32[8,128]{1,0:T(8,128)S(1)}, f32[8,128]{1,0:T(8,128)S(1)}) custom-call(bf16[128,4608]{1,0:T(8,128)(2,1)S(1)} %bitcast.38, bf16[128,4352]{1,0:T(8,128)(2,1)S(1)} %bitcast.41, f32[8,4096]{1,0:T(8,128)S(1)} %get-tuple-element.29.x_ref.refs_0_.refs_2_.refs_3_.refs_4_.refs_1_, ...), custom_call_target="tpu_custom_call" | custom-call | tf_op jit(solution)/shard_map/block2/pallas_call | solution.py:295
  100.1 16.9 %all_to_all.48 = bf16[16,8,4096]{2,1,0:T(8,128)(2,1)S(1)} all-to-all(bf16[16,8,4096]{2,1,0:T(8,128)(2,1)S(1)} %bitcast.55), channel_id=1, replica_groups={{0,2,4,6,14,12,10,18,20,22,30,28,26,24,16,8},{1,3,5,7,15,13,11,19,21,23..., dimensions={0} | all-to-all | bytes 2097152 | tf_op jit(solution)/shard_map/all_to_all | solution.py:261
  117.0 0.1 convert_reduce_fusion.2
  117.2 4.3 %collective-permute-done.7.before_ref = bf16[8,4096]{1,0:T(8,128)(2,1)S(1)} collective-permute-done((bf16[8,4096]{1,0:T(8,128)(2,1)S(1)}, bf16[8,4096]{1,0:T(8,128)(2,1)S(1)}, u32[]{:S(2)}, u32[]{:S(2)}) %collective-permute-start.7) | collective-permute-done | bytes 65568 | tf_op jit(solution)/shard_map/ppermute | solution.py:302
  121.5 0.2 image2.1
  121.7 4.8 %collective-permute-start.8 = (bf16[8,128]{1,0:T(8,128)(2,1)S(1)}, bf16[8,128]{1,0:T(8,128)(2,1)S(1)}, u32[]{:S(2)}, u32[]{:S(2)}) collective-permute-start(bf16[8,128]{1,0:T(8,128)(2,1)S(1)} %get-tuple-element.36), channel_id=1, source_target_pairs={{0,1},{1,0},{2,3},{3,2},{4,5},{5,4},{6,7},{7,6},{8,9},{9,8},{10,11... | collective-permute-start | bytes 6152 | tf_op jit(solution)/shard_map/ppermute | solution.py:311
  126.5 0.8 collective-permute-done.8
  127.4 20.5 %all_to_all.49 = bf16[16,8,4352]{2,1,0:T(8,128)(2,1)S(1)} all-to-all(bf16[16,8,4352]{2,1,0:T(8,128)(2,1)S(1)} %broadcast_in_dim.16), channel_id=1, replica_groups={{0,2,4,6,14,12,10,18,20,22,30,28,26,24,16,8},{1,3,5,7,15,13,11,19,21,23..., dimensions={0} | all-to-all | bytes 2228224 | tf_op jit(solution)/shard_map/all_to_all | solution.py:261
  147.9 5.8 %block3.1 = (bf16[128,4096]{1,0:T(8,128)(2,1)S(1)}, f32[8,4096]{1,0:T(8,128)S(1)}, f32[8,128]{1,0:T(8,128)S(1)}, f32[8,128]{1,0:T(8,128)S(1)}) custom-call(bf16[128,4608]{1,0:T(8,128)(2,1)S(1)} %bitcast.39, bf16[128,4352]{1,0:T(8,128)(2,1)S(1)} %bitcast.42, bf16[128,4352]{1,0:T(8,128)(2,1)S(1)} %bitcast.44, ...), custom_call_target="tpu_custom_call" | custom-call | tf_op jit(solution)/shard_map/block3/pallas_call | solution.py:295
  153.8 16.9 %all_to_all.50 = bf16[16,8,4096]{2,1,0:T(8,128)(2,1)S(1)} all-to-all(bf16[16,8,4096]{2,1,0:T(8,128)(2,1)S(1)} %bitcast.54), channel_id=1, replica_groups={{0,2,4,6,14,12,10,18,20,22,30,28,26,24,16,8},{1,3,5,7,15,13,11,19,21,23..., dimensions={0} | all-to-all | bytes 2097152 | tf_op jit(solution)/shard_map/all_to_all | solution.py:261
  170.6 0.1 convert_reduce_fusion.1
  170.9 4.3 %collective-permute-done.9.before_ref = bf16[8,4096]{1,0:T(8,128)(2,1)S(1)} collective-permute-done((bf16[8,4096]{1,0:T(8,128)(2,1)S(1)}, bf16[8,4096]{1,0:T(8,128)(2,1)S(1)}, u32[]{:S(2)}, u32[]{:S(2)}) %collective-permute-start.9) | collective-permute-done | bytes 65568 | tf_op jit(solution)/shard_map/ppermute | solution.py:302
  175.2 0.3 image3.1
  175.5 5.0 %collective-permute-start.10 = (bf16[8,128]{1,0:T(8,128)(2,1)S(1)}, bf16[8,128]{1,0:T(8,128)(2,1)S(1)}, u32[]{:S(2)}, u32[]{:S(2)}) collective-permute-start(bf16[8,128]{1,0:T(8,128)(2,1)S(1)} %get-tuple-element.42), channel_id=1, source_target_pairs={{0,1},{1,0},{2,3},{3,2},{4,5},{5,4},{6,7},{7,6},{8,9},{9,8},{10,11... | collective-permute-start | bytes 6152 | tf_op jit(solution)/shard_map/ppermute | solution.py:311
  180.5 0.8 collective-permute-done.10
  181.4 20.5 %all_to_all.51 = bf16[16,8,4352]{2,1,0:T(8,128)(2,1)S(1)} all-to-all(bf16[16,8,4352]{2,1,0:T(8,128)(2,1)S(1)} %broadcast_in_dim.17), channel_id=1, replica_groups={{0,2,4,6,14,12,10,18,20,22,30,28,26,24,16,8},{1,3,5,7,15,13,11,19,21,23..., dimensions={0} | all-to-all | bytes 2228224 | tf_op jit(solution)/shard_map/all_to_all | solution.py:261
  201.9 6.2 %block4.1 = (bf16[128,4096]{1,0:T(8,128)(2,1)S(1)}, f32[8,4096]{1,0:T(8,128)S(1)}, f32[8,128]{1,0:T(8,128)S(1)}, f32[8,128]{1,0:T(8,128)S(1)}) custom-call(bf16[128,4608]{1,0:T(8,128)(2,1)S(1)} %bitcast.40, bf16[128,4352]{1,0:T(8,128)(2,1)S(1)} %bitcast.43, bf16[128,4352]{1,0:T(8,128)(2,1)S(1)} %bitcast.45, bf16[128,4352]{1,0:T(8,128)(2,1)S(1)} %bitcast.46, ...), custom_call_target="tpu_custom_call" | custom-call | tf_op jit(solution)/shard_map/block4/pallas_call | solution.py:295
  208.1 16.9 %all_to_all.52 = bf16[16,8,4096]{2,1,0:T(8,128)(2,1)S(1)} all-to-all(bf16[16,8,4096]{2,1,0:T(8,128)(2,1)S(1)} %bitcast.53), channel_id=1, replica_groups={{0,2,4,6,14,12,10,18,20,22,30,28,26,24,16,8},{1,3,5,7,15,13,11,19,21,23..., dimensions={0} | all-to-all | bytes 2097152 | tf_op jit(solution)/shard_map/all_to_all | solution.py:261
  225.0 0.1 convert_reduce_fusion
  225.2 0.1 collective-permute-start.11
  225.3 4.3 %collective-permute-done.11.before_ref = bf16[8,4096]{1,0:T(8,128)(2,1)S(1)} collective-permute-done((bf16[8,4096]{1,0:T(8,128)(2,1)S(1)}, bf16[8,4096]{1,0:T(8,128)(2,1)S(1)}, u32[]{:S(2)}, u32[]{:S(2)}) %collective-permute-start.11) | collective-permute-done | bytes 65568 | tf_op jit(solution)/shard_map/ppermute | solution.py:302
  229.6 0.8 image4.1
  230.4 4.8 %collective-permute-start.12 = (bf16[8,128]{1,0:T(8,128)(2,1)S(1)}, bf16[8,128]{1,0:T(8,128)(2,1)S(1)}, u32[]{:S(2)}, u32[]{:S(2)}) collective-permute-start(bf16[8,128]{1,0:T(8,128)(2,1)S(1)} %get-tuple-element.48), channel_id=1, source_target_pairs={{0,1},{1,0},{2,3},{3,2},{4,5},{5,4},{6,7},{7,6},{8,9},{9,8},{10,11... | collective-permute-start | bytes 6152 | tf_op jit(solution)/shard_map/ppermute | solution.py:311
  235.1 0.8 collective-permute-done.12
  236.0 0.6 broadcast_in_dim.18
  236.6 3.6 %all-to-all-start.8 = ((bf16[16,8,256]{2,1,0:T(8,128)(2,1)}), bf16[16,8,256]{2,1,0:T(8,128)(2,1)S(1)}, u32[]{:S(2)}, u32[]{:S(2)}) async-start(bf16[16,8,256]{2,1,0:T(8,128)(2,1)} %broadcast_in_dim.18), calls=%async_computation.8 | async-start | bytes 131072 | tf_op jit(solution)/shard_map/all_to_all | solution.py:261
  240.2 6.5 %all-to-all-done.8 = bf16[16,8,256]{2,1,0:T(8,128)(2,1)S(1)} async-done(((bf16[16,8,256]{2,1,0:T(8,128)(2,1)}), bf16[16,8,256]{2,1,0:T(8,128)(2,1)S(1)}, u32[]{:S(2)}, u32[]{:S(2)}) %all-to-all-start.8) | async-done | bytes 65568 | tf_op jit(solution)/shard_map/all_to_all | solution.py:261
  246.7 1.7 final.1
  248.5 0.6 copy.7
  (39 shorter events, 0.8 us)
Async XLA Ops:
  0.6 41.3 %collective-permute-start.2 = (bf16[344,4096]{1,0:T(8,128)(2,1)}, bf16[344,4096]{1,0:T(8,128)(2,1)S(1)}, u32[]{:S(2)}, u32[]{:S(2)}) collective-permute-start(bf16[344,4096]{1,0:T(8,128)(2,1)} %bitcast.19), channel_id=1, source_target_pairs={{0,1},{1,0},{2,3},{3,2},{4,5},{5,4},{6,7},{7,6},{8,9},{9,8},{10,11... | collective-permute-start | bytes 8454152 | tf_op jit(solution)/shard_map/ppermute | solution.py:270
  3.9 38.0 %collective-permute-start.3 = (bf16[344,4096]{1,0:T(8,128)(2,1)}, bf16[344,4096]{1,0:T(8,128)(2,1)S(1)}, u32[]{:S(2)}, u32[]{:S(2)}) collective-permute-start(bf16[344,4096]{1,0:T(8,128)(2,1)} %bitcast.25), channel_id=1, source_target_pairs={{0,1},{1,0},{2,3},{3,2},{4,5},{5,4},{6,7},{7,6},{8,9},{9,8},{10,11... | collective-permute-start | bytes 8454152 | tf_op jit(solution)/shard_map/ppermute | solution.py:270
  4.0 37.9 %collective-permute-start.4 = (bf16[344,4096]{1,0:T(8,128)(2,1)}, bf16[344,4096]{1,0:T(8,128)(2,1)S(1)}, u32[]{:S(2)}, u32[]{:S(2)}) collective-permute-start(bf16[344,4096]{1,0:T(8,128)(2,1)} %bitcast.31), channel_id=1, source_target_pairs={{0,1},{1,0},{2,3},{3,2},{4,5},{5,4},{6,7},{7,6},{8,9},{9,8},{10,11... | collective-permute-start | bytes 8454152 | tf_op jit(solution)/shard_map/ppermute | solution.py:270
  4.4 1.8 copy-start
  6.2 1.8 copy-start.2
  8.0 1.8 copy-start.4
  9.8 0.7 copy-start.6
  10.5 7.4 %copy-start.5 = (bf16[1,8,4096]{2,1,0:T(8,128)(2,1)S(1)}, bf16[1,8,4096]{2,1,0:T(8,128)(2,1)}, u32[]{:S(2)}) copy-start(bf16[1,8,4096]{2,1,0:T(8,128)(2,1)} %param.5) | copy-start | bytes 196612
  10.5 31.4 %copy-start.3 = (bf16[1,4096,344]{1,2,0:T(8,128)(2,1)S(1)}, bf16[1,4096,344]{1,2,0:T(8,128)(2,1)}, u32[]{:S(2)}) copy-start(bf16[1,4096,344]{1,2,0:T(8,128)(2,1)} %param.7) | copy-start | bytes 8454148
  12.7 29.3 %copy-start.1 = (bf16[1,4096,344]{1,2,0:T(8,128)(2,1)S(1)}, bf16[1,4096,344]{1,2,0:T(8,128)(2,1)}, u32[]{:S(2)}) copy-start(bf16[1,4096,344]{1,2,0:T(8,128)(2,1)} %param.6) | copy-start | bytes 8454148
  12.7 29.3 %copy-start.7 = (f32[1,4096]{1,0:T(1,128)S(1)}, f32[1,4096]{1,0:T(1,128)}, u32[]{:S(2)}) copy-start(f32[1,4096]{1,0:T(1,128)} %refs_9_.1) | copy-start | bytes 49156
  12.7 5.3 %collective-permute-start.1 = (bf16[8,512]{1,0:T(8,128)(2,1)S(1)}, bf16[8,512]{1,0:T(8,128)(2,1)S(1)}, u32[]{:S(2)}, u32[]{:S(2)}) collective-permute-start(bf16[8,512]{1,0:T(8,128)(2,1)S(1)} %start.1), channel_id=1, source_target_pairs={{0,33},{1,32},{2,35},{3,34},{4,37},{5,36},{6,39},{7,38},{8,41},{9,... | collective-permute-start | bytes 24584 | tf_op jit(solution)/shard_map/ppermute | solution.py:273
  12.8 5.2 %collective-permute-start = (bf16[8,512]{1,0:T(8,128)(2,1)S(1)}, bf16[8,512]{1,0:T(8,128)(2,1)S(1)}, u32[]{:S(2)}, u32[]{:S(2)}) collective-permute-start(bf16[8,512]{1,0:T(8,128)(2,1)S(1)} %start.1), channel_id=1, source_target_pairs={{0,32},{32,64},{64,96},{96,128},{128,160},{160,192},{192,224},{224... | collective-permute-start | bytes 24584 | tf_op jit(solution)/shard_map/ppermute | solution.py:272
  64.0 4.4 %collective-permute-start.5 = (bf16[8,4096]{1,0:T(8,128)(2,1)S(1)}, bf16[8,4096]{1,0:T(8,128)(2,1)S(1)}, u32[]{:S(2)}, u32[]{:S(2)}) collective-permute-start(bf16[8,4096]{1,0:T(8,128)(2,1)S(1)} %add_convert_fusion.3), channel_id=1, source_target_pairs={{0,32},{32,64},{64,96},{96,128},{128,160},{160,192},{192,224},{224... | collective-permute-start | bytes 196616 | tf_op jit(solution)/shard_map/ppermute | solution.py:302
  68.6 5.3 %collective-permute-start.6 = (bf16[8,128]{1,0:T(8,128)(2,1)S(1)}, bf16[8,128]{1,0:T(8,128)(2,1)S(1)}, u32[]{:S(2)}, u32[]{:S(2)}) collective-permute-start(bf16[8,128]{1,0:T(8,128)(2,1)S(1)} %get-tuple-element.31), channel_id=1, source_target_pairs={{0,1},{1,0},{2,3},{3,2},{4,5},{5,4},{6,7},{7,6},{8,9},{9,8},{10,11... | collective-permute-start | bytes 6152 | tf_op jit(solution)/shard_map/ppermute | solution.py:311
  117.1 4.4 %collective-permute-start.7 = (bf16[8,4096]{1,0:T(8,128)(2,1)S(1)}, bf16[8,4096]{1,0:T(8,128)(2,1)S(1)}, u32[]{:S(2)}, u32[]{:S(2)}) collective-permute-start(bf16[8,4096]{1,0:T(8,128)(2,1)S(1)} %add_convert_fusion.2), channel_id=1, source_target_pairs={{0,32},{32,64},{64,96},{96,128},{128,160},{160,192},{192,224},{224... | collective-permute-start | bytes 196616 | tf_op jit(solution)/shard_map/ppermute | solution.py:302
  121.7 5.6 %collective-permute-start.8 = (bf16[8,128]{1,0:T(8,128)(2,1)S(1)}, bf16[8,128]{1,0:T(8,128)(2,1)S(1)}, u32[]{:S(2)}, u32[]{:S(2)}) collective-permute-start(bf16[8,128]{1,0:T(8,128)(2,1)S(1)} %get-tuple-element.36), channel_id=1, source_target_pairs={{0,1},{1,0},{2,3},{3,2},{4,5},{5,4},{6,7},{7,6},{8,9},{9,8},{10,11... | collective-permute-start | bytes 6152 | tf_op jit(solution)/shard_map/ppermute | solution.py:311
  170.8 4.4 %collective-permute-start.9 = (bf16[8,4096]{1,0:T(8,128)(2,1)S(1)}, bf16[8,4096]{1,0:T(8,128)(2,1)S(1)}, u32[]{:S(2)}, u32[]{:S(2)}) collective-permute-start(bf16[8,4096]{1,0:T(8,128)(2,1)S(1)} %add_convert_fusion.1), channel_id=1, source_target_pairs={{0,32},{32,64},{64,96},{96,128},{128,160},{160,192},{192,224},{224... | collective-permute-start | bytes 196616 | tf_op jit(solution)/shard_map/ppermute | solution.py:302
  175.5 5.8 %collective-permute-start.10 = (bf16[8,128]{1,0:T(8,128)(2,1)S(1)}, bf16[8,128]{1,0:T(8,128)(2,1)S(1)}, u32[]{:S(2)}, u32[]{:S(2)}) collective-permute-start(bf16[8,128]{1,0:T(8,128)(2,1)S(1)} %get-tuple-element.42), channel_id=1, source_target_pairs={{0,1},{1,0},{2,3},{3,2},{4,5},{5,4},{6,7},{7,6},{8,9},{9,8},{10,11... | collective-permute-start | bytes 6152 | tf_op jit(solution)/shard_map/ppermute | solution.py:311
  225.2 4.4 %collective-permute-start.11 = (bf16[8,4096]{1,0:T(8,128)(2,1)S(1)}, bf16[8,4096]{1,0:T(8,128)(2,1)S(1)}, u32[]{:S(2)}, u32[]{:S(2)}) collective-permute-start(bf16[8,4096]{1,0:T(8,128)(2,1)S(1)} %add_convert_fusion), channel_id=1, source_target_pairs={{0,32},{32,64},{64,96},{96,128},{128,160},{160,192},{192,224},{224... | collective-permute-start | bytes 196616 | tf_op jit(solution)/shard_map/ppermute | solution.py:302
  230.4 5.6 %collective-permute-start.12 = (bf16[8,128]{1,0:T(8,128)(2,1)S(1)}, bf16[8,128]{1,0:T(8,128)(2,1)S(1)}, u32[]{:S(2)}, u32[]{:S(2)}) collective-permute-start(bf16[8,128]{1,0:T(8,128)(2,1)S(1)} %get-tuple-element.48), channel_id=1, source_target_pairs={{0,1},{1,0},{2,3},{3,2},{4,5},{5,4},{6,7},{7,6},{8,9},{9,8},{10,11... | collective-permute-start | bytes 6152 | tf_op jit(solution)/shard_map/ppermute | solution.py:311
  236.6 10.1 %all-to-all-start.8 = ((bf16[16,8,256]{2,1,0:T(8,128)(2,1)}), bf16[16,8,256]{2,1,0:T(8,128)(2,1)S(1)}, u32[]{:S(2)}, u32[]{:S(2)}) async-start(bf16[16,8,256]{2,1,0:T(8,128)(2,1)} %broadcast_in_dim.18), calls=%async_computation.8 | async-start | bytes 131072 | tf_op jit(solution)/shard_map/all_to_all | solution.py:261
where the time goes:
time: 250 us; the launch traced here: 249 us
  blocking collectives  153 us (61%)
  waiting for transfers between devices  30.7 us (12%)
  starting transfers between devices  28.4 us (11%)
  Pallas kernels  27.6 us (11%)
  local copies, waits for them, and re-layouts  7.67 us (3%)
    all_to_all x8, blocking collectives, to_chips(): lax.all_to_all(array, 'dp', 0, 0, tiled=True, axis_index_groups=same_core)  153 us
    ppermute x4, starting transfers between devices, local(): payload = [extra, lax.ppermute(extra, 'dp', across)]  19.1 us
    pallas_call x3, Pallas kernels, local(): pallas(body, (part_shape, own_shape, small, small), f'block{iteration}',...  17.4 us
    ppermute x4, waiting for transfers between devices, local(): before = lax.ppermute((x + summed).astype(BF16), 'section', ahead)  17.3 us
    unnamed x17, local copies, waits for them, and re-layouts  6.7 us
    all_to_all x1, waiting for transfers between devices, to_chips(): lax.all_to_all(array, 'dp', 0, 0, tiled=True, axis_index_groups=same_core)  6.48 us
  transfers between devices with their start and end apart: 14, of which 10 were waited for; matrix products, arithmetic and copies ran while one was open for 0% of the time, Pallas kernels for 1%

commit v1 on v0

--- a/solution.py
+++ b/solution.py
@@ -11,7 +11,6 @@
 HIST = 5
 F32 = jnp.float32
 BF16 = jnp.bfloat16
-EXTRA = 256
 
 
 MIB = 1024 * 1024
@@ -22,13 +21,15 @@
 )
 
 
-def pallas(body, out_shape, name, limit, scratch=()):
+def pallas(body, out_shape, name, limit, scratch=(), places=None):
+    options = {} if places is None else {"in_specs": places}
     return pl.pallas_call(
         body,
         out_shape=out_shape,
         scratch_shapes=list(scratch),
         name=name,
         compiler_params=pltpu.CompilerParams(vmem_limit_bytes=limit * MIB),
+        **options,
     )
 
 
@@ -45,12 +46,20 @@
     return lax.dot_general(a, b, (((1,), (1,)), ((), ())), preferred_element_type=F32)
 
 
-def start_body(gain_ref, gate_ref, up_ref, down_ref, part_ref):
+def start_body(gain_ref, *refs):
+    sources, (part_ref, gate_ref, up_ref, down_ref, sems) = refs[:3], refs[3:]
+    held = (gate_ref, up_ref, down_ref)
+    copies = [pltpu.make_async_copy(sources[i], held[i], sems.at[i]) for i in range(3)]
+    for copy in copies:
+        copy.start()
     features = gate_ref.shape[1]
     normed = normalized(jnp.zeros((8, features), F32), gain_ref[...])
+    copies[0].wait()
     gate = by_rows(normed, gate_ref[...])
+    copies[1].wait()
     up = by_rows(normed, up_ref[...])
     act = silu_times(gate, up).astype(BF16)
+    copies[2].wait()
     piece = features // 8
     row = lax.broadcasted_iota(jnp.int32, (8, piece), 0)
     folded = jnp.zeros((8, piece), F32)
@@ -100,16 +109,12 @@
     return out
 
 
-def gram_and_weights(extras, state, iteration, cells):
-    chips = extras.shape[0] // 8
-    sums = extras[0:8].astype(F32)
-    for h in range(1, chips):
-        sums = sums + extras[8 * h : 8 * h + 8].astype(F32)
-    sums = sums[:, :128] + sums[:, 128:]
-    fresh = (sums[2:3] + sums[1:2] + sums[0:1]) / cells
-    known = [fresh] if state is None else [state[i : i + 1] for i in range(iteration)] + [fresh]
+def gram_and_weights(fresh, state, iteration, cells):
+    fresh = fresh[0:1] / cells
     if state is None:
         known = [lane_row([entry(fresh, 8)]), fresh]
+    else:
+        known = [state[i : i + 1] for i in range(iteration)] + [fresh]
     entries = [[None] * (iteration + 1) for _ in range(iteration + 1)]
     for i in range(iteration + 1):
         for j in range(i + 1):
@@ -151,90 +156,121 @@
         part_ref[:, cols] = part.astype(BF16)
 
 
-def first_block_body(first_ref, own_ref, gain_ref, *refs):
-    weights, (part_ref, image_ref, normed_ref) = refs[:6], refs[6:]
+def own_rows(x_ref, order):
+    chip = lax.axis_index("dp") // 2
+    slot = jnp.int32(0)
+    for i, h in enumerate(order):
+        slot = jnp.where(chip == h, i, slot)
+    return x_ref[pl.ds(pl.multiple_of(8 * slot, 8), 8), :]
+
+
+def first_block_body(order, first_ref, gain_ref, *refs):
+    weights, (part_ref, x_ref, own_x_ref, normed_ref) = refs[:6], refs[6:]
     tokens, features = part_ref.shape
     half = 0.5 * start_row(first_ref, features)
-    image_ref[...] = own_ref[...].astype(F32) + half
     for h in range(0, tokens, 16):
         rows = first_ref[h : h + 16, :features].astype(F32) + half
+        x_ref[h : h + 16, :] = rows
         normed_ref[h : h + 16, :] = normalized(rows, gain_ref[...])
+    own_x_ref[...] = own_rows(x_ref, order)
     send_block(normed_ref, weights, part_ref)
 
 
-def block_body(iteration, cells, *refs):
-    live = iteration
-    first_ref = refs[0]
-    outs = refs[1:live]
-    images = refs[live : 2 * live]
-    at = 2 * live
-    state_ref = None
+def block_body(iteration, cells, order, *refs):
+    own_ref, other_ref, first_ref = refs[:3]
+    outs = refs[3 : 2 + iteration]
+    at = 2 + iteration
+    state = None
     if iteration > 2:
-        state_ref = refs[at]
+        state = refs[at][...]
         at += 1
     gain_ref = refs[at]
     weights = refs[at + 1 : at + 7]
-    part_ref, x_ref, kept_ref, mix_ref, normed_ref = refs[at + 7 :]
+    if iteration < ITERS - 1:
+        part_ref, own_x_ref, kept_ref, mix_ref, x_ref, normed_ref = refs[at + 7 :]
+    else:
+        part_ref, own_x_ref, kept_ref, mix_ref, normed_ref, x_ref = refs[at + 7 :]
     tokens, features = part_ref.shape
-    state = None if state_ref is None else state_ref[...]
-    kept, mix, entries = gram_and_weights(outs[-1][:, features:], state, iteration - 1, cells)
+    fresh = own_ref[...] + other_ref[...]
+    kept, mix, entries = gram_and_weights(fresh, state, iteration - 1, cells)
     kept_ref[...] = kept
     mix_ref[...] = weight_rows(mix, entries, iteration == 2)
-    x = mix[0] * images[0][...]
-    for i in range(1, live):
-        x = x + mix[i] * images[i][...]
-    x_ref[...] = x
     total = mix[0]
-    for i in range(1, live):
+    for i in range(1, iteration):
         total = total + mix[i]
     base = (0.5 * mix[0]) * start_row(first_ref, features)
     for h in range(0, tokens, 16):
         rows = total * first_ref[h : h + 16, :features].astype(F32) + base
-        for i in range(1, live):
-            rows = rows + (0.5 * mix[i]) * outs[i - 1][h : h + 16, :features].astype(F32)
+        for i in range(1, iteration):
+            rows = rows + (0.5 * mix[i]) * outs[i - 1][h : h + 16, :].astype(F32)
+        x_ref[h : h + 16, :] = rows
         normed_ref[h : h + 16, :] = normalized(rows, gain_ref[...])
+    own_x_ref[...] = own_rows(x_ref, order)
     send_block(normed_ref, weights, part_ref)
 
 
-def split_in_three(values):
-    high = values.astype(BF16).astype(F32)
-    rest = values - high
-    mid = rest.astype(BF16).astype(F32)
-    low = rest - mid
-    return [high, mid, low]
-
-
-def inner(a, b):
-    return jnp.sum(jnp.sum(a * b, axis=0, keepdims=True), axis=1, keepdims=True)
-
-
-def image_body(iteration, before_ref, inject_ref, x_ref, *refs):
-    misfits = refs[:iteration]
-    image_ref, misfit_ref, extra_ref = refs[iteration:]
-    image = inject_ref[...].astype(F32) + 0.5 * before_ref[...].astype(F32)
-    misfit = image - x_ref[...]
-    image_ref[...] = image
-    misfit_ref[...] = misfit
-    values = [inner(misfit, misfits[j][...]) for j in range(iteration)] + [inner(misfit, misfit)]
-    row = lane_row(values)
-    if iteration == 1:
+def folded_lanes(values):
+    pieces = [values[:, n : n + 128] for n in range(0, values.shape[1], 128)]
+    while len(pieces) > 1:
+        pieces = [a + b for a, b in zip(pieces[::2], pieces[1::2])]
+    return pieces[0]
+
+
+def summed(values):
+    return jnp.sum(jnp.sum(values, axis=0, keepdims=True), axis=1, keepdims=True)
+
+
+def gram_row(sums, first):
+    row = lane_row([summed(s) for s in sums])
+    if first is not None:
         lane = lax.broadcasted_iota(jnp.int32, (1, 128), 1)
-        first = misfits[0][...]
-        row = row + jnp.where(lane == 8, inner(first, first), 0.0)
-    pieces = split_in_three(row)
-    extra_ref[...] = jnp.concatenate(pieces + [jnp.zeros((5, 128), F32)], axis=0).astype(BF16)
-
-
-def final_body(cells, *refs):
-    extra_ref = refs[0]
-    images = refs[1 : 1 + HIST]
-    state_ref = refs[1 + HIST]
-    x_ref, mix_ref = refs[2 + HIST :]
-    _, mix, entries = gram_and_weights(extra_ref[...], state_ref[...], ITERS - 1, cells)
+        row = row + jnp.where(lane == 8, summed(first), 0.0)
+    return jnp.concatenate([row, jnp.zeros((7, 128), F32)], axis=0)
+
+
+def misfit_body(iteration, first_ref, out_ref, x_ref, *refs):
+    befores = refs[:iteration]
+    row_ref, *kept = refs[iteration:]
+    tokens, features = x_ref.shape
+    sums = [jnp.zeros((8, 128), F32) for _ in range(iteration + 1)]
+    first = jnp.zeros((8, 128), F32)
+    for h in range(0, tokens, 16):
+        at = slice(h, h + 16)
+        image = first_ref[at, :features].astype(F32) + 0.5 * out_ref[at, :].astype(F32)
+        misfit = image - x_ref[at, :]
+        if kept:
+            kept[0][at, :] = misfit
+        for j in range(iteration + 1):
+            other = misfit if j == iteration else befores[j][at, :]
+            prod = folded_lanes(misfit * other)
+            sums[j] = sums[j] + prod[:8] + prod[8:]
+        if iteration == 1:
+            prod = folded_lanes(befores[0][at, :] * befores[0][at, :])
+            first = first + prod[:8] + prod[8:]
+    row_ref[...] = gram_row(sums, first if iteration == 1 else None)
+
+
+def last_misfit_body(inject_ref, *refs):
+    outs, xs, row_ref = refs[: ITERS - 1], refs[ITERS - 1 : -1], refs[-1]
+    inject = inject_ref[...].astype(F32)
+    misfits = [xs[0][...]]
+    for out_ref, x_ref in zip(outs, xs):
+        misfits.append(inject + 0.5 * out_ref[...].astype(F32) - x_ref[...])
+    row_ref[...] = gram_row([folded_lanes(misfits[-1] * m) for m in misfits], None)
+
+
+def final_body(cells, rows_ref, inject_ref, start_ref, state_ref, *refs):
+    outs, (x_ref, mix_ref) = refs[: ITERS - 1], refs[ITERS - 1 :]
+    fresh = rows_ref[0:8]
+    for h in range(8, rows_ref.shape[0], 8):
+        fresh = fresh + rows_ref[h : h + 8]
+    fresh = fresh[:, :128] + fresh[:, 128:]
+    _, mix, entries = gram_and_weights(fresh, state_ref[...], ITERS - 1, cells)
     mix_ref[...] = weight_rows(mix, entries, False)
-    x = mix[0] * images[0][...]
-    for i in range(1, HIST):
-        x = x + mix[i] * images[i][...]
+    inject = inject_ref[...].astype(F32)
+    x = mix[0] * start_ref[...]
+    for i in range(1, ITERS):
+        x = x + mix[i] * (inject + 0.5 * outs[i - 1][...].astype(F32))
     x_ref[...] = x
 
 
@@ -267,54 +303,66 @@
     shape = jax.ShapeDtypeStruct
     mine = inject[0]
     mine_w = [w_gate[0].T, w_up[0].T, w_down[0]]
-    other_w = [lax.ppermute(w, "dp", across) for w in mine_w]
-    part0 = pallas(start_body, shape((8, features // 8), BF16), "start", 12)(gain, *mine_w)
+    held = [pltpu.VMEM(w.shape, BF16) for w in mine_w] + [pltpu.SemaphoreType.DMA((3,))]
+    near_far = [pl.BlockSpec(memory_space=pltpu.VMEM)]
+    near_far += [pl.BlockSpec(memory_space=pltpu.HBM)] * 3
+    part0 = pallas(start_body, shape((8, features // 8), BF16), "start", 60, held, near_far)(
+        gain, *mine_w
+    )
+    part0, sent_w = lax.optimization_barrier((part0, mine_w))
+    other_w = [lax.ppermute(w, "dp", across) for w in sent_w]
     near = lax.ppermute(part0, "section", ahead)
     far = lax.ppermute(part0, both, ahead_across)
     start_part = (near.astype(F32) + far.astype(F32)).astype(BF16)
     first = to_all(jnp.concatenate([mine, start_part], axis=1))
 
     part_shape = shape((tokens, features), BF16)
+    wide_shape = shape((tokens, features), F32)
     own_shape = shape((rows, features), F32)
     small = shape((8, 128), F32)
     scratch = [pltpu.VMEM((tokens, features), BF16)]
     weights = mine_w + other_w
-    images, misfits, gathered, mixing = [], [], [], []
-    state = None
+    misfits, gathered, own_outs, own_xs, mixing = [], [], [], [], []
+    state = row = None
     for iteration in range(1, ITERS):
         if iteration == 1:
-            part, x = pallas(first_block_body, (part_shape, own_shape), "block1", 12, scratch)(
-                first, mine, gain, *weights
-            )
-            images.append(x)
+            body = functools.partial(first_block_body, order)
+            shapes = (part_shape, wide_shape, own_shape)
+            part, x, own_x = pallas(body, shapes, "block1", 12, scratch)(first, gain, *weights)
             misfits.append(x)
         else:
-            body = functools.partial(block_body, iteration, cells)
+            body = functools.partial(block_body, iteration, cells, order)
             carried = [] if state is None else [state]
-            arrays = (first, *gathered, *images, *carried, gain, *weights)
-            part, x, state, mix = pallas(
-                body, (part_shape, own_shape, small, small), f"block{iteration}", 12, scratch
-            )(first, *gathered, *images, *carried, gain, *weights)
+            other_row = lax.ppermute(row, "dp", across)
+            shapes = [part_shape, own_shape, small, small]
+            held = list(scratch)
+            if iteration < ITERS - 1:
+                shapes.append(wide_shape)
+            else:
+                held.append(pltpu.VMEM((tokens, features), F32))
+            part, own_x, state, mix, *rest = pallas(body, shapes, f"block{iteration}", 12, held)(
+                row, other_row, first, *gathered, *carried, gain, *weights
+            )
+            x = rest[0] if rest else None
             if iteration == 2:
                 mixing.append(mix[1, :HIST])
             mixing.append(mix[0, :HIST])
-        summed = jnp.sum(to_chips(part.reshape(chips, rows, features)).astype(F32), axis=0)
-        before = lax.ppermute((x + summed).astype(BF16), "section", ahead)
-        image, misfit, extra = pallas(
-            functools.partial(image_body, iteration),
-            (own_shape, own_shape, shape((8, 128), BF16)),
-            f"image{iteration}",
-            8,
-        )(before, mine, x, *misfits)
-        images.append(image)
-        misfits.append(misfit)
-        payload = [extra, lax.ppermute(extra, "dp", across)]
+        own_xs.append(own_x)
+        total = jnp.sum(to_chips(part.reshape(chips, rows, features)).astype(F32), axis=0)
+        before = lax.ppermute((own_xs[-1] + total).astype(BF16), "section", ahead)
+        own_outs.append(before)
         if iteration < ITERS - 1:
-            payload = [before] + payload
-        gathered.append(to_all(jnp.concatenate(payload, axis=1)))
-    iterate, mix = pallas(
-        functools.partial(final_body, cells), (shape((rows, features), F32), small), "final", 8
-    )(gathered[-1], *images, state)
+            gathered.append(to_all(before))
+            shapes = [small] + [wide_shape] * (iteration < ITERS - 2)
+            row, *misfit = pallas(
+                functools.partial(misfit_body, iteration), shapes, f"misfit{iteration}", 12
+            )(first, gathered[-1], x, *misfits)
+            misfits += misfit
+    row = pallas(last_misfit_body, small, "last_misfit", 8)(mine, *own_outs, *own_xs)
+    sums = to_all(jnp.concatenate([row, lax.ppermute(row, "dp", across)], axis=1))
+    iterate, mix = pallas(functools.partial(final_body, cells), (own_shape, small), "final", 8)(
+        sums, mine, own_xs[0], state, *own_outs
+    )
     mixing.append(mix[0, :HIST])
     return iterate[None], jnp.stack(mixing)[None]
 

time: 250 us -> 247 us (0.988)
  Pallas kernels: 27.6 us -> 35.9 us
  blocking collectives: 153 us -> 145 us
  local copies, waits for them, and re-layouts: 7.67 us -> 3.46 us
    pallas_call x10, Pallas kernels: 27.6 us -> 35.9 us  [the longest x3 18.3 us: local(): pallas(body, shapes, f'block{iteration}', 12, held)]
    all_to_all x8, blocking collectives: 153 us -> 145 us  [to_chips(): lax.all_to_all(array, 'dp', 0, 0, tiled=True, axis_index_groups=same_core)]
    unnamed x17 -> x13, local copies, waits for them, and re-layouts: 6.7 us -> 2.4 us
  transfers between devices with their start and end apart: 14 -> 14, of which waited for: 10 -> 10; matrix products, arithmetic and copies ran while one was open for 0% -> 0% of each run, Pallas kernels for 1% -> 0%
where the time goes in v1:
time: 247 us; the launch traced here: 246 us
  blocking collectives  145 us (59%)
  Pallas kernels  35.9 us (15%)
  waiting for transfers between devices  31.1 us (13%)
  starting transfers between devices  29.4 us (12%)
  local copies, waits for them, and re-layouts  3.46 us (1%)
    all_to_all x8, blocking collectives, to_chips(): lax.all_to_all(array, 'dp', 0, 0, tiled=True, axis_index_groups=same_core)  145 us
    pallas_call x3, Pallas kernels, local(): pallas(body, shapes, f'block{iteration}', 12, held)  18.3 us
    ppermute x4, waiting for transfers between devices, local(): before = lax.ppermute((own_xs[-1] + total).astype(BF16), 'section', ahead)  17.3 us
    ppermute x3, starting transfers between devices, local(): other_row = lax.ppermute(row, 'dp', across)  16.4 us
    pallas_call x1, Pallas kernels, local(): pallas(start_body, shape((8, features // 8), BF16), 'start', 60, held, ne...  6.72 us
    all_to_all x1, waiting for transfers between devices, to_chips(): lax.all_to_all(array, 'dp', 0, 0, tiled=True, axis_index_groups=same_core)  6.67 us
  transfers between devices with their start and end apart: 14, of which 10 were waited for; matrix products, arithmetic and copies ran while one was open for 0% of the time, Pallas kernels for 0%

profile of v1, /device:TPU:1, one launch (start us, length us, event | category | flops | bytes accessed | tf_op | source)
XLA Modules:
  0.0 246.4 jit_solution(11470053309256122918)
XLA Ops:
  0.6 6.7 %start.1 = bf16[8,512]{1,0:T(8,128)(2,1)} custom-call(f32[1,4096]{1,0:T(1,128)} %refs_7_.1, bf16[344,4096]{1,0:T(8,128)(2,1)} %bitcast.26, bf16[344,4096]{1,0:T(8,128)(2,1)} %bitcast.32, bf16[344,4096]{1,0:T(8,128)(2,1)} %bitcast.38), custom_call_target="tpu_custom_call" | custom-call | tf_op jit(solution)/shard_map/start/pallas_call | solution.py:309
  7.4 3.3 %collective-permute-start.2 = (bf16[344,4096]{1,0:T(8,128)(2,1)S(1)}, bf16[344,4096]{1,0:T(8,128)(2,1)S(1)}, u32[]{:S(2)}, u32[]{:S(2)}) collective-permute-start(bf16[344,4096]{1,0:T(8,128)(2,1)S(1)} %bitcast.27), channel_id=1, source_target_pairs={{0,1},{1,0},{2,3},{3,2},{4,5},{5,4},{6,7},{7,6},{8,9},{9,8},{10,11... | collective-permute-start | bytes 8454152 | tf_op jit(solution)/shard_map/ppermute | solution.py:313
  10.7 0.1 collective-permute-start.3
  10.8 0.4 collective-permute-start.4
  11.2 1.6 collective-permute-start
  12.8 3.9 %collective-permute-done.1 = bf16[8,512]{1,0:T(8,128)(2,1)S(1)} collective-permute-done((bf16[8,512]{1,0:T(8,128)(2,1)}, bf16[8,512]{1,0:T(8,128)(2,1)S(1)}, u32[]{:S(2)}, u32[]{:S(2)}) %collective-permute-start.1) | collective-permute-done | bytes 8224 | tf_op jit(solution)/shard_map/ppermute | solution.py:315
  16.7 23.9 %all_to_all.45 = bf16[16,8,4608]{2,1,0:T(8,128)(2,1)S(1)} all-to-all(bf16[16,8,4608]{2,1,0:T(8,128)(2,1)S(1)} %broadcast_in_dim.14), channel_id=1, replica_groups={{0,2,4,6,14,12,10,18,20,22,30,28,26,24,16,8},{1,3,5,7,15,13,11,19,21,23..., dimensions={0} | all-to-all | bytes 2359296 | tf_op jit(solution)/shard_map/all_to_all | solution.py:297
  40.7 1.8 copy-done.2
  42.4 4.9 %block1.1 = (bf16[128,4096]{1,0:T(8,128)(2,1)S(1)}, f32[128,4096]{1,0:T(8,128)S(1)}, f32[8,4096]{1,0:T(8,128)S(1)}) custom-call(bf16[128,4608]{1,0:T(8,128)(2,1)S(1)} %bitcast.19, f32[1,4096]{1,0:T(1,128)S(1)} %copy-done.5, bf16[344,4096]{1,0:T(8,128)(2,1)S(1)} %bitcast.28, bf16[344,4096]{1,0:T(8,128)(2,1)S(1)} %bitcast.34, bf16[344,4096]{1,0:T(8,128)(2,1)S(1)} %bitcast.40, ...), custom_call_target="tpu_custom_call" | custom-call | tf_op jit(solution)/shard_map/block1/pallas_call | solution.py:331
  47.3 17.0 %all_to_all.46 = bf16[16,8,4096]{2,1,0:T(8,128)(2,1)S(1)} all-to-all(bf16[16,8,4096]{2,1,0:T(8,128)(2,1)S(1)} %bitcast.56), channel_id=1, replica_groups={{0,2,4,6,14,12,10,18,20,22,30,28,26,24,16,8},{1,3,5,7,15,13,11,19,21,23..., dimensions={0} | all-to-all | bytes 2097152 | tf_op jit(solution)/shard_map/all_to_all | solution.py:297
  64.3 0.1 convert_reduce_fusion.3
  64.5 0.1 collective-permute-start.5
  64.6 4.3 %collective-permute-done.5.refs_0_ = bf16[8,4096]{1,0:T(8,128)(2,1)S(1)} collective-permute-done((bf16[8,4096]{1,0:T(8,128)(2,1)S(1)}, bf16[8,4096]{1,0:T(8,128)(2,1)S(1)}, u32[]{:S(2)}, u32[]{:S(2)}) %collective-permute-start.5) | collective-permute-done | bytes 65568 | tf_op jit(solution)/shard_map/ppermute | solution.py:352
  68.9 0.1 broadcast_in_dim.15
  69.0 15.3 %all_to_all.47 = bf16[16,8,4096]{2,1,0:T(8,128)(2,1)S(1)} all-to-all(bf16[16,8,4096]{2,1,0:T(8,128)(2,1)S(1)} %broadcast_in_dim.15), channel_id=1, replica_groups={{0,2,4,6,14,12,10,18,20,22,30,28,26,24,16,8},{1,3,5,7,15,13,11,19,21,23..., dimensions={0} | all-to-all | bytes 2097152 | tf_op jit(solution)/shard_map/all_to_all | solution.py:297
  84.3 1.2 misfit1.1
  85.5 6.2 %collective-permute-start.6 = (f32[8,128]{1,0:T(8,128)S(1)}, f32[8,128]{1,0:T(8,128)S(1)}, u32[]{:S(2)}, u32[]{:S(2)}) collective-permute-start(f32[8,128]{1,0:T(8,128)S(1)} %get-tuple-element.36.refs_0_), channel_id=1, source_target_pairs={{0,1},{1,0},{2,3},{3,2},{4,5},{5,4},{6,7},{7,6},{8,9},{9,8},{10,11... | collective-permute-start | bytes 12296 | tf_op jit(solution)/shard_map/ppermute | solution.py:336
  91.7 0.8 collective-permute-done.6.refs_1_
  92.5 5.5 %block2.1 = (bf16[128,4096]{1,0:T(8,128)(2,1)S(1)}, f32[8,4096]{1,0:T(8,128)S(1)}, f32[8,128]{1,0:T(8,128)S(1)}, f32[8,128]{1,0:T(8,128)S(1)}, f32[128,4096]{1,0:T(8,128)S(1)}) custom-call(f32[8,128]{1,0:T(8,128)S(1)} %get-tuple-element.36.refs_0_, f32[8,128]{1,0:T(8,128)S(1)} %collective-permute-done.6.refs_1_, bf16[128,4608]{1,0:T(8,128)(2,1)S(1)} %bitcast.21, ...), custom_call_target="tpu_custom_call" | custom-call | tf_op jit(solution)/shard_map/block2/pallas_call | solution.py:343
  98.1 18.4 %all_to_all.48 = bf16[16,8,4096]{2,1,0:T(8,128)(2,1)S(1)} all-to-all(bf16[16,8,4096]{2,1,0:T(8,128)(2,1)S(1)} %bitcast.55), channel_id=1, replica_groups={{0,2,4,6,14,12,10,18,20,22,30,28,26,24,16,8},{1,3,5,7,15,13,11,19,21,23..., dimensions={0} | all-to-all | bytes 2097152 | tf_op jit(solution)/shard_map/all_to_all | solution.py:297
  116.5 0.1 convert_reduce_fusion.2
  116.7 4.3 %collective-permute-done.7.refs_1_ = bf16[8,4096]{1,0:T(8,128)(2,1)S(1)} collective-permute-done((bf16[8,4096]{1,0:T(8,128)(2,1)S(1)}, bf16[8,4096]{1,0:T(8,128)(2,1)S(1)}, u32[]{:S(2)}, u32[]{:S(2)}) %collective-permute-start.7) | collective-permute-done | bytes 65568 | tf_op jit(solution)/shard_map/ppermute | solution.py:352
  121.1 0.1 broadcast_in_dim.16
  121.2 16.8 %all_to_all.49 = bf16[16,8,4096]{2,1,0:T(8,128)(2,1)S(1)} all-to-all(bf16[16,8,4096]{2,1,0:T(8,128)(2,1)S(1)} %broadcast_in_dim.16), channel_id=1, replica_groups={{0,2,4,6,14,12,10,18,20,22,30,28,26,24,16,8},{1,3,5,7,15,13,11,19,21,23..., dimensions={0} | all-to-all | bytes 2097152 | tf_op jit(solution)/shard_map/all_to_all | solution.py:297
  138.0 1.3 misfit2.1
  139.3 5.1 %collective-permute-start.8 = (f32[8,128]{1,0:T(8,128)S(1)}, f32[8,128]{1,0:T(8,128)S(1)}, u32[]{:S(2)}, u32[]{:S(2)}) collective-permute-start(f32[8,128]{1,0:T(8,128)S(1)} %get-tuple-element.41.refs_0_), channel_id=1, source_target_pairs={{0,1},{1,0},{2,3},{3,2},{4,5},{5,4},{6,7},{7,6},{8,9},{9,8},{10,11... | collective-permute-start | bytes 12296 | tf_op jit(solution)/shard_map/ppermute | solution.py:336
  144.4 0.8 collective-permute-done.8.refs_1_
  145.3 6.1 %block3.1 = (bf16[128,4096]{1,0:T(8,128)(2,1)S(1)}, f32[8,4096]{1,0:T(8,128)S(1)}, f32[8,128]{1,0:T(8,128)S(1)}, f32[8,128]{1,0:T(8,128)S(1)}, f32[128,4096]{1,0:T(8,128)S(1)}) custom-call(f32[8,128]{1,0:T(8,128)S(1)} %get-tuple-element.41.refs_0_, f32[8,128]{1,0:T(8,128)S(1)} %collective-permute-done.8.refs_1_, bf16[128,4608]{1,0:T(8,128)(2,1)S(1)} %bitcast.23, ...), custom_call_target="tpu_custom_call" | custom-call | tf_op jit(solution)/shard_map/block3/pallas_call | solution.py:343
  151.4 18.4 %all_to_all.50 = bf16[16,8,4096]{2,1,0:T(8,128)(2,1)S(1)} all-to-all(bf16[16,8,4096]{2,1,0:T(8,128)(2,1)S(1)} %bitcast.54), channel_id=1, replica_groups={{0,2,4,6,14,12,10,18,20,22,30,28,26,24,16,8},{1,3,5,7,15,13,11,19,21,23..., dimensions={0} | all-to-all | bytes 2097152 | tf_op jit(solution)/shard_map/all_to_all | solution.py:297
  169.8 0.1 convert_reduce_fusion.1
  170.0 4.3 %collective-permute-done.9.refs_2_ = bf16[8,4096]{1,0:T(8,128)(2,1)S(1)} collective-permute-done((bf16[8,4096]{1,0:T(8,128)(2,1)S(1)}, bf16[8,4096]{1,0:T(8,128)(2,1)S(1)}, u32[]{:S(2)}, u32[]{:S(2)}) %collective-permute-start.9) | collective-permute-done | bytes 65568 | tf_op jit(solution)/shard_map/ppermute | solution.py:352
  174.3 0.1 broadcast_in_dim.17
  174.4 16.8 %all_to_all.51 = bf16[16,8,4096]{2,1,0:T(8,128)(2,1)S(1)} all-to-all(bf16[16,8,4096]{2,1,0:T(8,128)(2,1)S(1)} %broadcast_in_dim.17), channel_id=1, replica_groups={{0,2,4,6,14,12,10,18,20,22,30,28,26,24,16,8},{1,3,5,7,15,13,11,19,21,23..., dimensions={0} | all-to-all | bytes 2097152 | tf_op jit(solution)/shard_map/all_to_all | solution.py:297
  191.2 1.5 misfit3.1.refs_0_
  192.8 5.1 %collective-permute-start.10 = (f32[8,128]{1,0:T(8,128)S(1)}, f32[8,128]{1,0:T(8,128)S(1)}, u32[]{:S(2)}, u32[]{:S(2)}) collective-permute-start(f32[8,128]{1,0:T(8,128)S(1)} %misfit3.1.refs_0_), channel_id=1, source_target_pairs={{0,1},{1,0},{2,3},{3,2},{4,5},{5,4},{6,7},{7,6},{8,9},{9,8},{10,11... | collective-permute-start | bytes 12296 | tf_op jit(solution)/shard_map/ppermute | solution.py:336
  197.9 0.8 collective-permute-done.10.refs_1_
  198.7 6.7 %block4.1 = (bf16[128,4096]{1,0:T(8,128)(2,1)S(1)}, f32[8,4096]{1,0:T(8,128)S(1)}, f32[8,128]{1,0:T(8,128)S(1)}, f32[8,128]{1,0:T(8,128)S(1)}) custom-call(f32[8,128]{1,0:T(8,128)S(1)} %misfit3.1.refs_0_, f32[8,128]{1,0:T(8,128)S(1)} %collective-permute-done.10.refs_1_, bf16[128,4608]{1,0:T(8,128)(2,1)S(1)} %bitcast.25, bf16[128,4096]{1,0:T(8,128)(2,1)S(1)} %bitcast.47, ...), custom_call_target="tpu_custom_call" | custom-call | tf_op jit(solution)/shard_map/block4/pallas_call | solution.py:343
  205.4 18.4 %all_to_all.52 = bf16[16,8,4096]{2,1,0:T(8,128)(2,1)S(1)} all-to-all(bf16[16,8,4096]{2,1,0:T(8,128)(2,1)S(1)} %bitcast.53), channel_id=1, replica_groups={{0,2,4,6,14,12,10,18,20,22,30,28,26,24,16,8},{1,3,5,7,15,13,11,19,21,23..., dimensions={0} | all-to-all | bytes 2097152 | tf_op jit(solution)/shard_map/all_to_all | solution.py:297
  223.8 0.1 convert_reduce_fusion
  224.1 4.3 %collective-permute-done.11.refs_3_ = bf16[8,4096]{1,0:T(8,128)(2,1)S(1)} collective-permute-done((bf16[8,4096]{1,0:T(8,128)(2,1)S(1)}, bf16[8,4096]{1,0:T(8,128)(2,1)S(1)}, u32[]{:S(2)}, u32[]{:S(2)}) %collective-permute-start.11) | collective-permute-done | bytes 65568 | tf_op jit(solution)/shard_map/ppermute | solution.py:352
  228.4 0.2 last_misfit.1
  228.6 3.8 %collective-permute-start.12 = (f32[8,128]{1,0:T(8,128)S(1)}, f32[8,128]{1,0:T(8,128)S(1)}, u32[]{:S(2)}, u32[]{:S(2)}) collective-permute-start(f32[8,128]{1,0:T(8,128)S(1)} %last_misfit.1), channel_id=1, source_target_pairs={{0,1},{1,0},{2,3},{3,2},{4,5},{5,4},{6,7},{7,6},{8,9},{9,8},{10,11... | collective-permute-start | bytes 12296 | tf_op jit(solution)/shard_map/ppermute | solution.py:362
  232.4 0.8 collective-permute-done.12
  233.2 0.7 broadcast_in_dim.18
  233.9 3.5 %all-to-all-start.8 = ((f32[16,8,256]{2,1,0:T(8,128)}), f32[16,8,256]{2,1,0:T(8,128)S(1)}, u32[]{:S(2)}, u32[]{:S(2)}) async-start(f32[16,8,256]{2,1,0:T(8,128)} %broadcast_in_dim.18), calls=%async_computation.8 | async-start | bytes 262144 | tf_op jit(solution)/shard_map/all_to_all | solution.py:297
  237.4 6.7 %all-to-all-done.8 = f32[16,8,256]{2,1,0:T(8,128)S(1)} async-done(((f32[16,8,256]{2,1,0:T(8,128)}), f32[16,8,256]{2,1,0:T(8,128)S(1)}, u32[]{:S(2)}, u32[]{:S(2)}) %all-to-all-start.8) | async-done | bytes 131104 | tf_op jit(solution)/shard_map/all_to_all | solution.py:297
  244.1 1.7 final.1
  245.9 0.6 copy.7
  (32 shorter events, 0.5 us)
Async XLA Ops:
  0.6 6.8 %copy-start = (bf16[1,4096,344]{1,2,0:T(8,128)(2,1)S(1)}, bf16[1,4096,344]{1,2,0:T(8,128)(2,1)}, u32[]{:S(2)}) copy-start(bf16[1,4096,344]{1,2,0:T(8,128)(2,1)} %param.6) | copy-start | bytes 8454148
  0.6 16.0 %copy-start.4 = (bf16[1,8,4096]{2,1,0:T(8,128)(2,1)S(1)}, bf16[1,8,4096]{2,1,0:T(8,128)(2,1)}, u32[]{:S(2)}) copy-start(bf16[1,8,4096]{2,1,0:T(8,128)(2,1)} %param.5) | copy-start | bytes 196612
  7.4 33.2 %copy-start.1 = (bf16[1,4096,344]{1,2,0:T(8,128)(2,1)S(1)}, bf16[1,4096,344]{1,2,0:T(8,128)(2,1)}, u32[]{:S(2)}) copy-start(bf16[1,4096,344]{1,2,0:T(8,128)(2,1)} %param.7) | copy-start | bytes 8454148
  7.4 33.2 %copy-start.5 = (f32[1,4096]{1,0:T(1,128)S(1)}, f32[1,4096]{1,0:T(1,128)}, u32[]{:S(2)}) copy-start(f32[1,4096]{1,0:T(1,128)} %refs_7_.1) | copy-start | bytes 49156
  7.4 33.2 %collective-permute-start.2 = (bf16[344,4096]{1,0:T(8,128)(2,1)S(1)}, bf16[344,4096]{1,0:T(8,128)(2,1)S(1)}, u32[]{:S(2)}, u32[]{:S(2)}) collective-permute-start(bf16[344,4096]{1,0:T(8,128)(2,1)S(1)} %bitcast.27), channel_id=1, source_target_pairs={{0,1},{1,0},{2,3},{3,2},{4,5},{5,4},{6,7},{7,6},{8,9},{9,8},{10,11... | collective-permute-start | bytes 8454152 | tf_op jit(solution)/shard_map/ppermute | solution.py:313
  10.7 29.9 %collective-permute-start.3 = (bf16[344,4096]{1,0:T(8,128)(2,1)}, bf16[344,4096]{1,0:T(8,128)(2,1)S(1)}, u32[]{:S(2)}, u32[]{:S(2)}) collective-permute-start(bf16[344,4096]{1,0:T(8,128)(2,1)} %bitcast.33), channel_id=1, source_target_pairs={{0,1},{1,0},{2,3},{3,2},{4,5},{5,4},{6,7},{7,6},{8,9},{9,8},{10,11... | collective-permute-start | bytes 8454152 | tf_op jit(solution)/shard_map/ppermute | solution.py:313
  10.8 29.8 %collective-permute-start.4 = (bf16[344,4096]{1,0:T(8,128)(2,1)}, bf16[344,4096]{1,0:T(8,128)(2,1)S(1)}, u32[]{:S(2)}, u32[]{:S(2)}) collective-permute-start(bf16[344,4096]{1,0:T(8,128)(2,1)} %bitcast.39), channel_id=1, source_target_pairs={{0,1},{1,0},{2,3},{3,2},{4,5},{5,4},{6,7},{7,6},{8,9},{9,8},{10,11... | collective-permute-start | bytes 8454152 | tf_op jit(solution)/shard_map/ppermute | solution.py:313
  11.2 5.4 %collective-permute-start.1 = (bf16[8,512]{1,0:T(8,128)(2,1)}, bf16[8,512]{1,0:T(8,128)(2,1)S(1)}, u32[]{:S(2)}, u32[]{:S(2)}) collective-permute-start(bf16[8,512]{1,0:T(8,128)(2,1)} %start.1), channel_id=1, source_target_pairs={{0,33},{1,32},{2,35},{3,34},{4,37},{5,36},{6,39},{7,38},{8,41},{9,... | collective-permute-start | bytes 24584 | tf_op jit(solution)/shard_map/ppermute | solution.py:315
  11.2 5.4 %collective-permute-start = (bf16[8,512]{1,0:T(8,128)(2,1)}, bf16[8,512]{1,0:T(8,128)(2,1)S(1)}, u32[]{:S(2)}, u32[]{:S(2)}) collective-permute-start(bf16[8,512]{1,0:T(8,128)(2,1)} %start.1), channel_id=1, source_target_pairs={{0,32},{32,64},{64,96},{96,128},{128,160},{160,192},{192,224},{224... | collective-permute-start | bytes 24584 | tf_op jit(solution)/shard_map/ppermute | solution.py:314
  40.6 1.8 copy-start.2
  64.5 4.4 %collective-permute-start.5 = (bf16[8,4096]{1,0:T(8,128)(2,1)S(1)}, bf16[8,4096]{1,0:T(8,128)(2,1)S(1)}, u32[]{:S(2)}, u32[]{:S(2)}) collective-permute-start(bf16[8,4096]{1,0:T(8,128)(2,1)S(1)} %add_convert_fusion.3), channel_id=1, source_target_pairs={{0,32},{32,64},{64,96},{96,128},{128,160},{160,192},{192,224},{224... | collective-permute-start | bytes 196616 | tf_op jit(solution)/shard_map/ppermute | solution.py:352
  84.3 8.2 %copy-start.3 = (bf16[1,344,4096]{2,1,0:T(8,128)(2,1)S(1)}, bf16[1,344,4096]{2,1,0:T(8,128)(2,1)}, u32[]{:S(2)}) copy-start(bf16[1,344,4096]{2,1,0:T(8,128)(2,1)} %param.8) | copy-start | bytes 8454148
  85.5 7.0 %collective-permute-start.6 = (f32[8,128]{1,0:T(8,128)S(1)}, f32[8,128]{1,0:T(8,128)S(1)}, u32[]{:S(2)}, u32[]{:S(2)}) collective-permute-start(f32[8,128]{1,0:T(8,128)S(1)} %get-tuple-element.36.refs_0_), channel_id=1, source_target_pairs={{0,1},{1,0},{2,3},{3,2},{4,5},{5,4},{6,7},{7,6},{8,9},{9,8},{10,11... | collective-permute-start | bytes 12296 | tf_op jit(solution)/shard_map/ppermute | solution.py:336
  116.6 4.4 %collective-permute-start.7 = (bf16[8,4096]{1,0:T(8,128)(2,1)S(1)}, bf16[8,4096]{1,0:T(8,128)(2,1)S(1)}, u32[]{:S(2)}, u32[]{:S(2)}) collective-permute-start(bf16[8,4096]{1,0:T(8,128)(2,1)S(1)} %add_convert_fusion.2), channel_id=1, source_target_pairs={{0,32},{32,64},{64,96},{96,128},{128,160},{160,192},{192,224},{224... | collective-permute-start | bytes 196616 | tf_op jit(solution)/shard_map/ppermute | solution.py:352
  139.3 6.0 %collective-permute-start.8 = (f32[8,128]{1,0:T(8,128)S(1)}, f32[8,128]{1,0:T(8,128)S(1)}, u32[]{:S(2)}, u32[]{:S(2)}) collective-permute-start(f32[8,128]{1,0:T(8,128)S(1)} %get-tuple-element.41.refs_0_), channel_id=1, source_target_pairs={{0,1},{1,0},{2,3},{3,2},{4,5},{5,4},{6,7},{7,6},{8,9},{9,8},{10,11... | collective-permute-start | bytes 12296 | tf_op jit(solution)/shard_map/ppermute | solution.py:336
  169.9 4.4 %collective-permute-start.9 = (bf16[8,4096]{1,0:T(8,128)(2,1)S(1)}, bf16[8,4096]{1,0:T(8,128)(2,1)S(1)}, u32[]{:S(2)}, u32[]{:S(2)}) collective-permute-start(bf16[8,4096]{1,0:T(8,128)(2,1)S(1)} %add_convert_fusion.1), channel_id=1, source_target_pairs={{0,32},{32,64},{64,96},{96,128},{128,160},{160,192},{192,224},{224... | collective-permute-start | bytes 196616 | tf_op jit(solution)/shard_map/ppermute | solution.py:352
  192.8 5.9 %collective-permute-start.10 = (f32[8,128]{1,0:T(8,128)S(1)}, f32[8,128]{1,0:T(8,128)S(1)}, u32[]{:S(2)}, u32[]{:S(2)}) collective-permute-start(f32[8,128]{1,0:T(8,128)S(1)} %misfit3.1.refs_0_), channel_id=1, source_target_pairs={{0,1},{1,0},{2,3},{3,2},{4,5},{5,4},{6,7},{7,6},{8,9},{9,8},{10,11... | collective-permute-start | bytes 12296 | tf_op jit(solution)/shard_map/ppermute | solution.py:336
  224.0 4.4 %collective-permute-start.11 = (bf16[8,4096]{1,0:T(8,128)(2,1)S(1)}, bf16[8,4096]{1,0:T(8,128)(2,1)S(1)}, u32[]{:S(2)}, u32[]{:S(2)}) collective-permute-start(bf16[8,4096]{1,0:T(8,128)(2,1)S(1)} %add_convert_fusion), channel_id=1, source_target_pairs={{0,32},{32,64},{64,96},{96,128},{128,160},{160,192},{192,224},{224... | collective-permute-start | bytes 196616 | tf_op jit(solution)/shard_map/ppermute | solution.py:352
  228.6 4.6 %collective-permute-start.12 = (f32[8,128]{1,0:T(8,128)S(1)}, f32[8,128]{1,0:T(8,128)S(1)}, u32[]{:S(2)}, u32[]{:S(2)}) collective-permute-start(f32[8,128]{1,0:T(8,128)S(1)} %last_misfit.1), channel_id=1, source_target_pairs={{0,1},{1,0},{2,3},{3,2},{4,5},{5,4},{6,7},{7,6},{8,9},{9,8},{10,11... | collective-permute-start | bytes 12296 | tf_op jit(solution)/shard_map/ppermute | solution.py:362
  233.9 10.2 %all-to-all-start.8 = ((f32[16,8,256]{2,1,0:T(8,128)}), f32[16,8,256]{2,1,0:T(8,128)S(1)}, u32[]{:S(2)}, u32[]{:S(2)}) async-start(f32[16,8,256]{2,1,0:T(8,128)} %broadcast_in_dim.18), calls=%async_computation.8 | async-start | bytes 262144 | tf_op jit(solution)/shard_map/all_to_all | solution.py:297

commit v2 on v1

--- a/solution.py
+++ b/solution.py
@@ -21,15 +21,14 @@
 )
 
 
-def pallas(body, out_shape, name, limit, scratch=(), places=None):
-    options = {} if places is None else {"in_specs": places}
+def pallas(body, out_shape, name, limit, scratch=(), cost=None):
     return pl.pallas_call(
         body,
         out_shape=out_shape,
         scratch_shapes=list(scratch),
         name=name,
+        cost_estimate=cost,
         compiler_params=pltpu.CompilerParams(vmem_limit_bytes=limit * MIB),
-        **options,
     )
 
 
@@ -46,20 +45,12 @@
     return lax.dot_general(a, b, (((1,), (1,)), ((), ())), preferred_element_type=F32)
 
 
-def start_body(gain_ref, *refs):
-    sources, (part_ref, gate_ref, up_ref, down_ref, sems) = refs[:3], refs[3:]
-    held = (gate_ref, up_ref, down_ref)
-    copies = [pltpu.make_async_copy(sources[i], held[i], sems.at[i]) for i in range(3)]
-    for copy in copies:
-        copy.start()
+def start_body(gain_ref, gate_ref, up_ref, down_ref, part_ref):
     features = gate_ref.shape[1]
     normed = normalized(jnp.zeros((8, features), F32), gain_ref[...])
-    copies[0].wait()
     gate = by_rows(normed, gate_ref[...])
-    copies[1].wait()
     up = by_rows(normed, up_ref[...])
     act = silu_times(gate, up).astype(BF16)
-    copies[2].wait()
     piece = features // 8
     row = lax.broadcasted_iota(jnp.int32, (8, piece), 0)
     folded = jnp.zeros((8, piece), F32)
@@ -141,18 +132,39 @@
     return jnp.concatenate([sums[r : r + 1] for r in range(8)], axis=1)
 
 
-def send_block(normed_ref, weights, part_ref):
+def products(rows_ref, weights, pre_ref):
+    for i, w_ref in enumerate(weights):
+        hidden = w_ref.shape[0]
+        pre_ref[i * hidden : (i + 1) * hidden] = by_rows(w_ref[...], rows_ref[...])
+
+
+def products_body(rows_ref, *refs):
+    products(rows_ref, refs[:4], refs[4])
+
+
+def lane_rsqrt(squares_ref, features):
+    mean = jnp.transpose(squares_ref[...])[:1] * (1.0 / features)
+    return lax.rsqrt(mean + 1e-06)
+
+
+def squares_of(rows):
+    sums = jnp.sum(rows * rows, axis=1, keepdims=True)
+    return jnp.broadcast_to(sums, (rows.shape[0], 128))
+
+
+def send_block(pre, factor, downs, part_ref):
+    hidden = downs[0].shape[0]
     acts = []
-    for gate_ref, up_ref in (weights[0:2], weights[3:5]):
-        gate = by_rows(gate_ref[...], normed_ref[...])
-        up = by_rows(up_ref[...], normed_ref[...])
+    for half in range(2):
+        gate = pre(2 * half * hidden, hidden) * factor
+        up = pre((2 * half + 1) * hidden, hidden) * factor
         acts.append(jnp.transpose(silu_times(gate, up)).astype(BF16))
     features = part_ref.shape[1]
     step = min(512, features)
     for n in range(0, features, step):
         cols = slice(n, n + step)
-        part = jnp.dot(acts[0], weights[2][:, cols], preferred_element_type=F32)
-        part = part + jnp.dot(acts[1], weights[5][:, cols], preferred_element_type=F32)
+        part = jnp.dot(acts[0], downs[0][:, cols], preferred_element_type=F32)
+        part = part + jnp.dot(acts[1], downs[1][:, cols], preferred_element_type=F32)
         part_ref[:, cols] = part.astype(BF16)
 
 
@@ -165,31 +177,35 @@
 
 
 def first_block_body(order, first_ref, gain_ref, *refs):
-    weights, (part_ref, x_ref, own_x_ref, normed_ref) = refs[:6], refs[6:]
+    weights, downs = refs[:4], refs[4:6]
+    part_ref, x_ref, own_x_ref, pre_ref, scaled_ref, squares_ref = refs[6:]
     tokens, features = part_ref.shape
     half = 0.5 * start_row(first_ref, features)
     for h in range(0, tokens, 16):
         rows = first_ref[h : h + 16, :features].astype(F32) + half
         x_ref[h : h + 16, :] = rows
-        normed_ref[h : h + 16, :] = normalized(rows, gain_ref[...])
+        scaled_ref[h : h + 16, :] = (rows * gain_ref[...]).astype(BF16)
+        squares_ref[h : h + 16, :] = squares_of(rows)
     own_x_ref[...] = own_rows(x_ref, order)
-    send_block(normed_ref, weights, part_ref)
+    products(scaled_ref, weights, pre_ref)
+    factor = lane_rsqrt(squares_ref, features)
+    send_block(lambda at, size: pre_ref[at : at + size], factor, downs, part_ref)
 
 
 def block_body(iteration, cells, order, *refs):
     own_ref, other_ref, first_ref = refs[:3]
     outs = refs[3 : 2 + iteration]
-    at = 2 + iteration
+    pres = refs[2 + iteration : 2 + 2 * iteration]
+    at = 2 + 2 * iteration
     state = None
     if iteration > 2:
         state = refs[at][...]
         at += 1
-    gain_ref = refs[at]
-    weights = refs[at + 1 : at + 7]
+    downs = refs[at : at + 2]
     if iteration < ITERS - 1:
-        part_ref, own_x_ref, kept_ref, mix_ref, x_ref, normed_ref = refs[at + 7 :]
+        part_ref, own_x_ref, kept_ref, mix_ref, x_ref, squares_ref = refs[at + 2 :]
     else:
-        part_ref, own_x_ref, kept_ref, mix_ref, normed_ref, x_ref = refs[at + 7 :]
+        part_ref, own_x_ref, kept_ref, mix_ref, squares_ref, x_ref = refs[at + 2 :]
     tokens, features = part_ref.shape
     fresh = own_ref[...] + other_ref[...]
     kept, mix, entries = gram_and_weights(fresh, state, iteration - 1, cells)
@@ -204,9 +220,17 @@
         for i in range(1, iteration):
             rows = rows + (0.5 * mix[i]) * outs[i - 1][h : h + 16, :].astype(F32)
         x_ref[h : h + 16, :] = rows
-        normed_ref[h : h + 16, :] = normalized(rows, gain_ref[...])
+        squares_ref[h : h + 16, :] = squares_of(rows)
     own_x_ref[...] = own_rows(x_ref, order)
-    send_block(normed_ref, weights, part_ref)
+    factor = lane_rsqrt(squares_ref, features)
+
+    def mixed(start, size):
+        accum = mix[0] * pres[0][start : start + size]
+        for i in range(1, iteration):
+            accum = accum + mix[i] * pres[i][start : start + size]
+        return accum
+
+    send_block(mixed, factor, downs, part_ref)
 
 
 def folded_lanes(values):
@@ -228,15 +252,16 @@
     return jnp.concatenate([row, jnp.zeros((7, 128), F32)], axis=0)
 
 
-def misfit_body(iteration, first_ref, out_ref, x_ref, *refs):
+def misfit_body(iteration, first_ref, out_ref, x_ref, gain_ref, *refs):
     befores = refs[:iteration]
-    row_ref, *kept = refs[iteration:]
+    row_ref, scaled_ref, *kept = refs[iteration:]
     tokens, features = x_ref.shape
     sums = [jnp.zeros((8, 128), F32) for _ in range(iteration + 1)]
     first = jnp.zeros((8, 128), F32)
     for h in range(0, tokens, 16):
         at = slice(h, h + 16)
         image = first_ref[at, :features].astype(F32) + 0.5 * out_ref[at, :].astype(F32)
+        scaled_ref[at, :] = (image * gain_ref[...]).astype(BF16)
         misfit = image - x_ref[at, :]
         if kept:
             kept[0][at, :] = misfit
@@ -264,7 +289,6 @@
     fresh = rows_ref[0:8]
     for h in range(8, rows_ref.shape[0], 8):
         fresh = fresh + rows_ref[h : h + 8]
-    fresh = fresh[:, :128] + fresh[:, 128:]
     _, mix, entries = gram_and_weights(fresh, state_ref[...], ITERS - 1, cells)
     mix_ref[...] = weight_rows(mix, entries, False)
     inject = inject_ref[...].astype(F32)
@@ -303,14 +327,8 @@
     shape = jax.ShapeDtypeStruct
     mine = inject[0]
     mine_w = [w_gate[0].T, w_up[0].T, w_down[0]]
-    held = [pltpu.VMEM(w.shape, BF16) for w in mine_w] + [pltpu.SemaphoreType.DMA((3,))]
-    near_far = [pl.BlockSpec(memory_space=pltpu.VMEM)]
-    near_far += [pl.BlockSpec(memory_space=pltpu.HBM)] * 3
-    part0 = pallas(start_body, shape((8, features // 8), BF16), "start", 60, held, near_far)(
-        gain, *mine_w
-    )
-    part0, sent_w = lax.optimization_barrier((part0, mine_w))
-    other_w = [lax.ppermute(w, "dp", across) for w in sent_w]
+    part0 = pallas(start_body, shape((8, features // 8), BF16), "start", 12)(gain, *mine_w)
+    other_w = [lax.ppermute(w, "dp", across) for w in mine_w]
     near = lax.ppermute(part0, "section", ahead)
     far = lax.ppermute(part0, both, ahead_across)
     start_part = (near.astype(F32) + far.astype(F32)).astype(BF16)
@@ -320,28 +338,46 @@
     wide_shape = shape((tokens, features), F32)
     own_shape = shape((rows, features), F32)
     small = shape((8, 128), F32)
-    scratch = [pltpu.VMEM((tokens, features), BF16)]
-    weights = mine_w + other_w
+    scaled_shape = shape((tokens, features), BF16)
+    pre_shape = shape((4 * hidden, tokens), F32)
+    squares = pltpu.VMEM((tokens, 128), F32)
+    weights = [mine_w[0], mine_w[1], other_w[0], other_w[1]]
+    downs = [mine_w[2], other_w[2]]
+    pres = []
+    cost = pl.CostEstimate(
+        flops=8 * hidden * tokens * features,
+        bytes_accessed=8 * hidden * features,
+        transcendentals=0,
+    )
     misfits, gathered, own_outs, own_xs, mixing = [], [], [], [], []
     state = row = None
     for iteration in range(1, ITERS):
         if iteration == 1:
             body = functools.partial(first_block_body, order)
-            shapes = (part_shape, wide_shape, own_shape)
-            part, x, own_x = pallas(body, shapes, "block1", 12, scratch)(first, gain, *weights)
+            shapes = (part_shape, wide_shape, own_shape, pre_shape)
+            held = [pltpu.VMEM((tokens, features), BF16), squares]
+            part, x, own_x, pre = pallas(body, shapes, "block1", 12, held)(
+                first, gain, *weights, *downs
+            )
+            pres.append(pre)
             misfits.append(x)
         else:
             body = functools.partial(block_body, iteration, cells, order)
             carried = [] if state is None else [state]
             other_row = lax.ppermute(row, "dp", across)
+            pres.append(
+                pallas(products_body, pre_shape, f"products{iteration}", 12, cost=cost)(
+                    scaled, *weights
+                )
+            )
             shapes = [part_shape, own_shape, small, small]
-            held = list(scratch)
+            held = [squares]
             if iteration < ITERS - 1:
                 shapes.append(wide_shape)
             else:
                 held.append(pltpu.VMEM((tokens, features), F32))
             part, own_x, state, mix, *rest = pallas(body, shapes, f"block{iteration}", 12, held)(
-                row, other_row, first, *gathered, *carried, gain, *weights
+                row, other_row, first, *gathered, *pres, *carried, *downs
             )
             x = rest[0] if rest else None
             if iteration == 2:
@@ -353,13 +389,14 @@
         own_outs.append(before)
         if iteration < ITERS - 1:
             gathered.append(to_all(before))
-            shapes = [small] + [wide_shape] * (iteration < ITERS - 2)
-            row, *misfit = pallas(
+            shapes = [small, scaled_shape] + [wide_shape] * (iteration < ITERS - 2)
+            row, scaled, *misfit = pallas(
                 functools.partial(misfit_body, iteration), shapes, f"misfit{iteration}", 12
-            )(first, gathered[-1], x, *misfits)
+            )(first, gathered[-1], x, gain, *misfits)
             misfits += misfit
     row = pallas(last_misfit_body, small, "last_misfit", 8)(mine, *own_outs, *own_xs)
-    sums = to_all(jnp.concatenate([row, lax.ppermute(row, "dp", across)], axis=1))
+    copies = jnp.broadcast_to(row[None], (groups, *row.shape))
+    sums = lax.all_to_all(copies, "dp", 0, 0, tiled=True).reshape(8 * groups, 128)
     iterate, mix = pallas(functools.partial(final_body, cells), (own_shape, small), "final", 8)(
         sums, mine, own_xs[0], state, *own_outs
     )

time: 247 us -> 244 us (0.988)
  local copies, waits for them, and re-layouts: 3.46 us -> 7.76 us
  Pallas kernels: 35.9 us -> 31.6 us
  waiting for transfers between devices: 31.1 us -> 28.6 us
    pallas_call x3, Pallas kernels: 18.3 us -> 9.42 us  [local(): pallas(body, shapes, f'block{iteration}', 12, held)]
    pallas_call x2 -> x5, Pallas kernels: 11.6 us -> 15.9 us  [the longest x3 9.34 us: local(): pallas(products_body, pre_shape, f'products{iteration}', 12, cost=cost)]
    unnamed x13 -> x19, local copies, waits for them, and re-layouts: 2.4 us -> 6.7 us
    all_to_all x1, starting transfers between devices: 3.51 us -> 7.34 us  [local(): lax.all_to_all(copies, 'dp', 0, 0, tiled=True).reshape(8 * groups, 128)]
    ppermute x4 -> x3, starting transfers between devices: 7.58 us -> 3.8 us  [local(): other_w = [lax.ppermute(w, 'dp', across) for w in mine_w]]
  transfers between devices with their start and end apart: 14 -> 13, of which waited for: 10 -> 6; matrix products, arithmetic and copies ran while one was open for 0% -> 0% of each run, Pallas kernels for 0% -> 5%
where the time goes in v2:
time: 244 us
  blocking collectives  145 us (59%)
  Pallas kernels  31.6 us (13%)
  starting transfers between devices  29.2 us (12%)
  waiting for transfers between devices  28.6 us (12%)
  local copies, waits for them, and re-layouts  7.76 us (3%)
    all_to_all x8, blocking collectives, to_chips(): lax.all_to_all(array, 'dp', 0, 0, tiled=True, axis_index_groups=same_core)  145 us
    ppermute x4, waiting for transfers between devices, local(): before = lax.ppermute((own_xs[-1] + total).astype(BF16), 'section', ahead)  17.3 us
    ppermute x3, starting transfers between devices, local(): other_row = lax.ppermute(row, 'dp', across)  16.1 us
    pallas_call x3, Pallas kernels, local(): pallas(body, shapes, f'block{iteration}', 12, held)  9.42 us
    pallas_call x3, Pallas kernels, local(): pallas(products_body, pre_shape, f'products{iteration}', 12, cost=cost)  9.34 us
    all_to_all x1, waiting for transfers between devices, local(): lax.all_to_all(copies, 'dp', 0, 0, tiled=True).reshape(8 * groups, 128)  7.64 us
    all_to_all x1, starting transfers between devices, local(): lax.all_to_all(copies, 'dp', 0, 0, tiled=True).reshape(8 * groups, 128)  7.34 us
    unnamed x19, local copies, waits for them, and re-layouts  6.7 us
  transfers between devices with their start and end apart: 13, of which 6 were waited for; matrix products, arithmetic and copies ran while one was open for 0% of the time, Pallas kernels for 5%

profile of v2, /device:TPU:1, one launch (start us, length us, event | category | flops | bytes accessed | tf_op | source)
XLA Modules:
  0.0 243.8 jit_solution(14108404443052551807)
XLA Ops:
  0.6 3.3 %collective-permute-start.2 = (bf16[344,4096]{1,0:T(8,128)(2,1)}, bf16[344,4096]{1,0:T(8,128)(2,1)S(1)}, u32[]{:S(2)}, u32[]{:S(2)}) collective-permute-start(bf16[344,4096]{1,0:T(8,128)(2,1)} %bitcast.26), channel_id=1, source_target_pairs={{0,1},{1,0},{2,3},{3,2},{4,5},{5,4},{6,7},{7,6},{8,9},{9,8},{10,11... | collective-permute-start | bytes 8454152 | tf_op jit(solution)/shard_map/ppermute | solution.py:331
  3.9 0.1 collective-permute-start.3
  4.0 0.4 collective-permute-start.4
  4.4 1.8 copy-done
  6.2 1.8 copy-done.2
  8.0 1.8 copy-done.4
  9.8 0.7 copy-done.7
  10.5 2.1 start.1
  12.8 1.5 collective-permute-start
  14.3 3.7 %collective-permute-done.1 = bf16[8,512]{1,0:T(8,128)(2,1)S(1)} collective-permute-done((bf16[8,512]{1,0:T(8,128)(2,1)S(1)}, bf16[8,512]{1,0:T(8,128)(2,1)S(1)}, u32[]{:S(2)}, u32[]{:S(2)}) %collective-permute-start.1) | collective-permute-done | bytes 8224 | tf_op jit(solution)/shard_map/ppermute | solution.py:333
  18.1 23.9 %all_to_all.45 = bf16[16,8,4608]{2,1,0:T(8,128)(2,1)S(1)} all-to-all(bf16[16,8,4608]{2,1,0:T(8,128)(2,1)S(1)} %broadcast_in_dim.14), channel_id=1, replica_groups={{0,2,4,6,14,12,10,18,20,22,30,28,26,24,16,8},{1,3,5,7,15,13,11,19,21,23..., dimensions={0} | all-to-all | bytes 2359296 | tf_op jit(solution)/shard_map/all_to_all | solution.py:321
  42.0 4.5 %block1.1 = (bf16[128,4096]{1,0:T(8,128)(2,1)S(1)}, f32[128,4096]{1,0:T(8,128)S(1)}, f32[8,4096]{1,0:T(8,128)S(1)}, f32[1376,128]{1,0:T(8,128)S(1)}) custom-call(bf16[128,4608]{1,0:T(8,128)(2,1)S(1)} %bitcast.19, f32[1,4096]{1,0:T(1,128)S(1)} %copy-done.8, bf16[344,4096]{1,0:T(8,128)(2,1)S(1)} %bitcast.28, bf16[344,4096]{1,0:T(8,128)(2,1)S(1)} %bitcast.34, ...), custom_call_target="tpu_custom_call" | custom-call | tf_op jit(solution)/shard_map/block1/pallas_call | solution.py:359
  46.4 17.0 %all_to_all.46 = bf16[16,8,4096]{2,1,0:T(8,128)(2,1)S(1)} all-to-all(bf16[16,8,4096]{2,1,0:T(8,128)(2,1)S(1)} %bitcast.56), channel_id=1, replica_groups={{0,2,4,6,14,12,10,18,20,22,30,28,26,24,16,8},{1,3,5,7,15,13,11,19,21,23..., dimensions={0} | all-to-all | bytes 2097152 | tf_op jit(solution)/shard_map/all_to_all | solution.py:321
  63.5 0.1 convert_reduce_fusion.3
  63.7 4.3 %collective-permute-done.5.refs_0_ = bf16[8,4096]{1,0:T(8,128)(2,1)S(1)} collective-permute-done((bf16[8,4096]{1,0:T(8,128)(2,1)S(1)}, bf16[8,4096]{1,0:T(8,128)(2,1)S(1)}, u32[]{:S(2)}, u32[]{:S(2)}) %collective-permute-start.5) | collective-permute-done | bytes 65568 | tf_op jit(solution)/shard_map/ppermute | solution.py:388
  68.1 0.1 broadcast_in_dim.15
  68.2 15.3 %all_to_all.47 = bf16[16,8,4096]{2,1,0:T(8,128)(2,1)S(1)} all-to-all(bf16[16,8,4096]{2,1,0:T(8,128)(2,1)S(1)} %broadcast_in_dim.15), channel_id=1, replica_groups={{0,2,4,6,14,12,10,18,20,22,30,28,26,24,16,8},{1,3,5,7,15,13,11,19,21,23..., dimensions={0} | all-to-all | bytes 2097152 | tf_op jit(solution)/shard_map/all_to_all | solution.py:321
  83.4 1.3 misfit1.1
  84.8 6.2 %collective-permute-start.6 = (f32[8,128]{1,0:T(8,128)S(1)}, f32[8,128]{1,0:T(8,128)S(1)}, u32[]{:S(2)}, u32[]{:S(2)}) collective-permute-start(f32[8,128]{1,0:T(8,128)S(1)} %get-tuple-element.33.refs_0_), channel_id=1, source_target_pairs={{0,1},{1,0},{2,3},{3,2},{4,5},{5,4},{6,7},{7,6},{8,9},{9,8},{10,11... | collective-permute-start | bytes 12296 | tf_op jit(solution)/shard_map/ppermute | solution.py:367
  90.9 3.1 %products2.1.refs_5_.refs_6_.refs_7_ = f32[1376,128]{1,0:T(8,128)S(1)} custom-call(bf16[128,4096]{1,0:T(8,128)(2,1)S(1)} %get-tuple-element.35.rows_ref, bf16[344,4096]{1,0:T(8,128)(2,1)S(1)} %bitcast.29, bf16[344,4096]{1,0:T(8,128)(2,1)S(1)} %bitcast.35, bf16[344,4096]{1,0:T(8,128)(2,1)S(1)} %collective-permute-done.2.refs_2_, ...), custom_call_target="tpu_custom_call" | custom-call | flops 1442840576 | bytes 11272192 | tf_op jit(solution)/shard_map/products2/pallas_call | solution.py:369
  94.1 2.5 %block2.1 = (bf16[128,4096]{1,0:T(8,128)(2,1)S(1)}, f32[8,4096]{1,0:T(8,128)S(1)}, f32[8,128]{1,0:T(8,128)S(1)}, f32[8,128]{1,0:T(8,128)S(1)}, f32[128,4096]{1,0:T(8,128)S(1)}) custom-call(f32[8,128]{1,0:T(8,128)S(1)} %get-tuple-element.33.refs_0_, f32[8,128]{1,0:T(8,128)S(1)} %collective-permute-done.6.refs_1_, bf16[128,4608]{1,0:T(8,128)(2,1)S(1)} %bitcast.21, ...), custom_call_target="tpu_custom_call" | custom-call | tf_op jit(solution)/shard_map/block2/pallas_call | solution.py:379
  96.6 18.7 %all_to_all.48 = bf16[16,8,4096]{2,1,0:T(8,128)(2,1)S(1)} all-to-all(bf16[16,8,4096]{2,1,0:T(8,128)(2,1)S(1)} %bitcast.55), channel_id=1, replica_groups={{0,2,4,6,14,12,10,18,20,22,30,28,26,24,16,8},{1,3,5,7,15,13,11,19,21,23..., dimensions={0} | all-to-all | bytes 2097152 | tf_op jit(solution)/shard_map/all_to_all | solution.py:321
  115.3 0.1 convert_reduce_fusion.2
  115.5 4.3 %collective-permute-done.7.refs_1_ = bf16[8,4096]{1,0:T(8,128)(2,1)S(1)} collective-permute-done((bf16[8,4096]{1,0:T(8,128)(2,1)S(1)}, bf16[8,4096]{1,0:T(8,128)(2,1)S(1)}, u32[]{:S(2)}, u32[]{:S(2)}) %collective-permute-start.7) | collective-permute-done | bytes 65568 | tf_op jit(solution)/shard_map/ppermute | solution.py:388
  119.8 0.1 broadcast_in_dim.16
  119.9 16.5 %all_to_all.49 = bf16[16,8,4096]{2,1,0:T(8,128)(2,1)S(1)} all-to-all(bf16[16,8,4096]{2,1,0:T(8,128)(2,1)S(1)} %broadcast_in_dim.16), channel_id=1, replica_groups={{0,2,4,6,14,12,10,18,20,22,30,28,26,24,16,8},{1,3,5,7,15,13,11,19,21,23..., dimensions={0} | all-to-all | bytes 2097152 | tf_op jit(solution)/shard_map/all_to_all | solution.py:321
  136.5 1.4 misfit2.1
  137.9 5.0 %collective-permute-start.8 = (f32[8,128]{1,0:T(8,128)S(1)}, f32[8,128]{1,0:T(8,128)S(1)}, u32[]{:S(2)}, u32[]{:S(2)}) collective-permute-start(f32[8,128]{1,0:T(8,128)S(1)} %get-tuple-element.40.refs_0_), channel_id=1, source_target_pairs={{0,1},{1,0},{2,3},{3,2},{4,5},{5,4},{6,7},{7,6},{8,9},{9,8},{10,11... | collective-permute-start | bytes 12296 | tf_op jit(solution)/shard_map/ppermute | solution.py:367
  142.9 3.1 %products3.1.refs_7_.refs_8_ = f32[1376,128]{1,0:T(8,128)S(1)} custom-call(bf16[128,4096]{1,0:T(8,128)(2,1)S(1)} %get-tuple-element.41.rows_ref, bf16[344,4096]{1,0:T(8,128)(2,1)S(1)} %bitcast.30, bf16[344,4096]{1,0:T(8,128)(2,1)S(1)} %bitcast.36, bf16[344,4096]{1,0:T(8,128)(2,1)S(1)} %collective-permute-done.2.refs_2_, ...), custom_call_target="tpu_custom_call" | custom-call | flops 1442840576 | bytes 11272192 | tf_op jit(solution)/shard_map/products3/pallas_call | solution.py:369
  146.0 3.1 %block3.1 = (bf16[128,4096]{1,0:T(8,128)(2,1)S(1)}, f32[8,4096]{1,0:T(8,128)S(1)}, f32[8,128]{1,0:T(8,128)S(1)}, f32[8,128]{1,0:T(8,128)S(1)}, f32[128,4096]{1,0:T(8,128)S(1)}) custom-call(f32[8,128]{1,0:T(8,128)S(1)} %get-tuple-element.40.refs_0_, f32[8,128]{1,0:T(8,128)S(1)} %collective-permute-done.8.refs_1_, bf16[128,4608]{1,0:T(8,128)(2,1)S(1)} %bitcast.23, ...), custom_call_target="tpu_custom_call" | custom-call | tf_op jit(solution)/shard_map/block3/pallas_call | solution.py:379
  149.1 18.6 %all_to_all.50 = bf16[16,8,4096]{2,1,0:T(8,128)(2,1)S(1)} all-to-all(bf16[16,8,4096]{2,1,0:T(8,128)(2,1)S(1)} %bitcast.54), channel_id=1, replica_groups={{0,2,4,6,14,12,10,18,20,22,30,28,26,24,16,8},{1,3,5,7,15,13,11,19,21,23..., dimensions={0} | all-to-all | bytes 2097152 | tf_op jit(solution)/shard_map/all_to_all | solution.py:321
  167.8 0.1 convert_reduce_fusion.1
  168.0 4.3 %collective-permute-done.9.refs_2_ = bf16[8,4096]{1,0:T(8,128)(2,1)S(1)} collective-permute-done((bf16[8,4096]{1,0:T(8,128)(2,1)S(1)}, bf16[8,4096]{1,0:T(8,128)(2,1)S(1)}, u32[]{:S(2)}, u32[]{:S(2)}) %collective-permute-start.9) | collective-permute-done | bytes 65568 | tf_op jit(solution)/shard_map/ppermute | solution.py:388
  172.3 0.1 broadcast_in_dim.17
  172.4 16.6 %all_to_all.51 = bf16[16,8,4096]{2,1,0:T(8,128)(2,1)S(1)} all-to-all(bf16[16,8,4096]{2,1,0:T(8,128)(2,1)S(1)} %broadcast_in_dim.17), channel_id=1, replica_groups={{0,2,4,6,14,12,10,18,20,22,30,28,26,24,16,8},{1,3,5,7,15,13,11,19,21,23..., dimensions={0} | all-to-all | bytes 2097152 | tf_op jit(solution)/shard_map/all_to_all | solution.py:321
  189.0 1.5 misfit3.1
  190.6 5.0 %collective-permute-start.10 = (f32[8,128]{1,0:T(8,128)S(1)}, f32[8,128]{1,0:T(8,128)S(1)}, u32[]{:S(2)}, u32[]{:S(2)}) collective-permute-start(f32[8,128]{1,0:T(8,128)S(1)} %get-tuple-element.47.refs_0_), channel_id=1, source_target_pairs={{0,1},{1,0},{2,3},{3,2},{4,5},{5,4},{6,7},{7,6},{8,9},{9,8},{10,11... | collective-permute-start | bytes 12296 | tf_op jit(solution)/shard_map/ppermute | solution.py:367
  195.5 3.1 %products4.1.refs_9_ = f32[1376,128]{1,0:T(8,128)S(1)} custom-call(bf16[128,4096]{1,0:T(8,128)(2,1)S(1)} %get-tuple-element.48.rows_ref, bf16[344,4096]{1,0:T(8,128)(2,1)S(1)} %bitcast.31, bf16[344,4096]{1,0:T(8,128)(2,1)S(1)} %bitcast.37, bf16[344,4096]{1,0:T(8,128)(2,1)S(1)} %collective-permute-done.2.refs_2_, ...), custom_call_target="tpu_custom_call" | custom-call | flops 1442840576 | bytes 11272192 | tf_op jit(solution)/shard_map/products4/pallas_call | solution.py:369
  198.6 3.7 %block4.1 = (bf16[128,4096]{1,0:T(8,128)(2,1)S(1)}, f32[8,4096]{1,0:T(8,128)S(1)}, f32[8,128]{1,0:T(8,128)S(1)}, f32[8,128]{1,0:T(8,128)S(1)}) custom-call(f32[8,128]{1,0:T(8,128)S(1)} %get-tuple-element.47.refs_0_, f32[8,128]{1,0:T(8,128)S(1)} %collective-permute-done.10.refs_1_, bf16[128,4608]{1,0:T(8,128)(2,1)S(1)} %bitcast.25, ...), custom_call_target="tpu_custom_call" | custom-call | tf_op jit(solution)/shard_map/block4/pallas_call | solution.py:379
  202.4 18.6 %all_to_all.52 = bf16[16,8,4096]{2,1,0:T(8,128)(2,1)S(1)} all-to-all(bf16[16,8,4096]{2,1,0:T(8,128)(2,1)S(1)} %bitcast.53), channel_id=1, replica_groups={{0,2,4,6,14,12,10,18,20,22,30,28,26,24,16,8},{1,3,5,7,15,13,11,19,21,23..., dimensions={0} | all-to-all | bytes 2097152 | tf_op jit(solution)/shard_map/all_to_all | solution.py:321
  221.0 0.1 convert_reduce_fusion
  221.3 4.3 %collective-permute-done.11.refs_3_ = bf16[8,4096]{1,0:T(8,128)(2,1)S(1)} collective-permute-done((bf16[8,4096]{1,0:T(8,128)(2,1)S(1)}, bf16[8,4096]{1,0:T(8,128)(2,1)S(1)}, u32[]{:S(2)}, u32[]{:S(2)}) %collective-permute-start.11) | collective-permute-done | bytes 65568 | tf_op jit(solution)/shard_map/ppermute | solution.py:388
  225.6 0.2 last_misfit.1
  225.8 0.7 broadcast_in_dim.18
  226.5 7.3 %all-to-all-start.8 = ((f32[32,8,128]{2,1,0:T(8,128)}), f32[32,8,128]{2,1,0:T(8,128)S(1)}, u32[]{:S(2)}, u32[]{:S(2)}) async-start(f32[32,8,128]{2,1,0:T(8,128)} %broadcast_in_dim.18), calls=%async_computation.8 | async-start | bytes 262144 | tf_op jit(solution)/shard_map/all_to_all | solution.py:399
  233.9 7.6 %all-to-all-done.8 = f32[32,8,128]{2,1,0:T(8,128)S(1)} async-done(((f32[32,8,128]{2,1,0:T(8,128)}), f32[32,8,128]{2,1,0:T(8,128)S(1)}, u32[]{:S(2)}, u32[]{:S(2)}) %all-to-all-start.8) | async-done | bytes 131104 | tf_op jit(solution)/shard_map/all_to_all | solution.py:399
  241.5 1.7 final.1
  243.3 0.6 copy.7
  (38 shorter events, 0.6 us)
Async XLA Ops:
  0.6 41.3 %collective-permute-start.2 = (bf16[344,4096]{1,0:T(8,128)(2,1)}, bf16[344,4096]{1,0:T(8,128)(2,1)S(1)}, u32[]{:S(2)}, u32[]{:S(2)}) collective-permute-start(bf16[344,4096]{1,0:T(8,128)(2,1)} %bitcast.26), channel_id=1, source_target_pairs={{0,1},{1,0},{2,3},{3,2},{4,5},{5,4},{6,7},{7,6},{8,9},{9,8},{10,11... | collective-permute-start | bytes 8454152 | tf_op jit(solution)/shard_map/ppermute | solution.py:331
  3.9 38.0 %collective-permute-start.3 = (bf16[344,4096]{1,0:T(8,128)(2,1)}, bf16[344,4096]{1,0:T(8,128)(2,1)S(1)}, u32[]{:S(2)}, u32[]{:S(2)}) collective-permute-start(bf16[344,4096]{1,0:T(8,128)(2,1)} %bitcast.32), channel_id=1, source_target_pairs={{0,1},{1,0},{2,3},{3,2},{4,5},{5,4},{6,7},{7,6},{8,9},{9,8},{10,11... | collective-permute-start | bytes 8454152 | tf_op jit(solution)/shard_map/ppermute | solution.py:331
  4.0 37.9 %collective-permute-start.4 = (bf16[344,4096]{1,0:T(8,128)(2,1)}, bf16[344,4096]{1,0:T(8,128)(2,1)S(1)}, u32[]{:S(2)}, u32[]{:S(2)}) collective-permute-start(bf16[344,4096]{1,0:T(8,128)(2,1)} %bitcast.38), channel_id=1, source_target_pairs={{0,1},{1,0},{2,3},{3,2},{4,5},{5,4},{6,7},{7,6},{8,9},{9,8},{10,11... | collective-permute-start | bytes 8454152 | tf_op jit(solution)/shard_map/ppermute | solution.py:331
  4.4 1.8 copy-start
  6.2 1.8 copy-start.2
  8.0 1.8 copy-start.4
  9.8 0.7 copy-start.7
  10.5 7.4 %copy-start.6 = (bf16[1,8,4096]{2,1,0:T(8,128)(2,1)S(1)}, bf16[1,8,4096]{2,1,0:T(8,128)(2,1)}, u32[]{:S(2)}) copy-start(bf16[1,8,4096]{2,1,0:T(8,128)(2,1)} %param.5) | copy-start | bytes 196612
  10.5 31.4 %copy-start.3 = (bf16[1,4096,344]{1,2,0:T(8,128)(2,1)S(1)}, bf16[1,4096,344]{1,2,0:T(8,128)(2,1)}, u32[]{:S(2)}) copy-start(bf16[1,4096,344]{1,2,0:T(8,128)(2,1)} %param.7) | copy-start | bytes 8454148
  12.7 29.3 %copy-start.1 = (bf16[1,4096,344]{1,2,0:T(8,128)(2,1)S(1)}, bf16[1,4096,344]{1,2,0:T(8,128)(2,1)}, u32[]{:S(2)}) copy-start(bf16[1,4096,344]{1,2,0:T(8,128)(2,1)} %param.6) | copy-start | bytes 8454148
  12.7 29.3 %copy-start.8 = (f32[1,4096]{1,0:T(1,128)S(1)}, f32[1,4096]{1,0:T(1,128)}, u32[]{:S(2)}) copy-start(f32[1,4096]{1,0:T(1,128)} %gain_ref.9) | copy-start | bytes 49156
  12.7 5.3 %collective-permute-start.1 = (bf16[8,512]{1,0:T(8,128)(2,1)S(1)}, bf16[8,512]{1,0:T(8,128)(2,1)S(1)}, u32[]{:S(2)}, u32[]{:S(2)}) collective-permute-start(bf16[8,512]{1,0:T(8,128)(2,1)S(1)} %start.1), channel_id=1, source_target_pairs={{0,33},{1,32},{2,35},{3,34},{4,37},{5,36},{6,39},{7,38},{8,41},{9,... | collective-permute-start | bytes 24584 | tf_op jit(solution)/shard_map/ppermute | solution.py:333
  12.8 5.2 %collective-permute-start = (bf16[8,512]{1,0:T(8,128)(2,1)S(1)}, bf16[8,512]{1,0:T(8,128)(2,1)S(1)}, u32[]{:S(2)}, u32[]{:S(2)}) collective-permute-start(bf16[8,512]{1,0:T(8,128)(2,1)S(1)} %start.1), channel_id=1, source_target_pairs={{0,32},{32,64},{64,96},{96,128},{128,160},{160,192},{192,224},{224... | collective-permute-start | bytes 24584 | tf_op jit(solution)/shard_map/ppermute | solution.py:332
  63.6 4.4 %collective-permute-start.5 = (bf16[8,4096]{1,0:T(8,128)(2,1)S(1)}, bf16[8,4096]{1,0:T(8,128)(2,1)S(1)}, u32[]{:S(2)}, u32[]{:S(2)}) collective-permute-start(bf16[8,4096]{1,0:T(8,128)(2,1)S(1)} %add_convert_fusion.3), channel_id=1, source_target_pairs={{0,32},{32,64},{64,96},{96,128},{128,160},{160,192},{192,224},{224... | collective-permute-start | bytes 196616 | tf_op jit(solution)/shard_map/ppermute | solution.py:388
  84.8 9.3 %collective-permute-start.6 = (f32[8,128]{1,0:T(8,128)S(1)}, f32[8,128]{1,0:T(8,128)S(1)}, u32[]{:S(2)}, u32[]{:S(2)}) collective-permute-start(f32[8,128]{1,0:T(8,128)S(1)} %get-tuple-element.33.refs_0_), channel_id=1, source_target_pairs={{0,1},{1,0},{2,3},{3,2},{4,5},{5,4},{6,7},{7,6},{8,9},{9,8},{10,11... | collective-permute-start | bytes 12296 | tf_op jit(solution)/shard_map/ppermute | solution.py:367
  90.9 3.1 %copy-start.5 = (bf16[1,344,4096]{2,1,0:T(8,128)(2,1)S(1)}, bf16[1,344,4096]{2,1,0:T(8,128)(2,1)}, u32[]{:S(2)}) copy-start(bf16[1,344,4096]{2,1,0:T(8,128)(2,1)} %param.8) | copy-start | bytes 8454148
  115.4 4.4 %collective-permute-start.7 = (bf16[8,4096]{1,0:T(8,128)(2,1)S(1)}, bf16[8,4096]{1,0:T(8,128)(2,1)S(1)}, u32[]{:S(2)}, u32[]{:S(2)}) collective-permute-start(bf16[8,4096]{1,0:T(8,128)(2,1)S(1)} %add_convert_fusion.2), channel_id=1, source_target_pairs={{0,32},{32,64},{64,96},{96,128},{128,160},{160,192},{192,224},{224... | collective-permute-start | bytes 196616 | tf_op jit(solution)/shard_map/ppermute | solution.py:388
  137.9 8.1 %collective-permute-start.8 = (f32[8,128]{1,0:T(8,128)S(1)}, f32[8,128]{1,0:T(8,128)S(1)}, u32[]{:S(2)}, u32[]{:S(2)}) collective-permute-start(f32[8,128]{1,0:T(8,128)S(1)} %get-tuple-element.40.refs_0_), channel_id=1, source_target_pairs={{0,1},{1,0},{2,3},{3,2},{4,5},{5,4},{6,7},{7,6},{8,9},{9,8},{10,11... | collective-permute-start | bytes 12296 | tf_op jit(solution)/shard_map/ppermute | solution.py:367
  167.9 4.4 %collective-permute-start.9 = (bf16[8,4096]{1,0:T(8,128)(2,1)S(1)}, bf16[8,4096]{1,0:T(8,128)(2,1)S(1)}, u32[]{:S(2)}, u32[]{:S(2)}) collective-permute-start(bf16[8,4096]{1,0:T(8,128)(2,1)S(1)} %add_convert_fusion.1), channel_id=1, source_target_pairs={{0,32},{32,64},{64,96},{96,128},{128,160},{160,192},{192,224},{224... | collective-permute-start | bytes 196616 | tf_op jit(solution)/shard_map/ppermute | solution.py:388
  190.6 8.1 %collective-permute-start.10 = (f32[8,128]{1,0:T(8,128)S(1)}, f32[8,128]{1,0:T(8,128)S(1)}, u32[]{:S(2)}, u32[]{:S(2)}) collective-permute-start(f32[8,128]{1,0:T(8,128)S(1)} %get-tuple-element.47.refs_0_), channel_id=1, source_target_pairs={{0,1},{1,0},{2,3},{3,2},{4,5},{5,4},{6,7},{7,6},{8,9},{9,8},{10,11... | collective-permute-start | bytes 12296 | tf_op jit(solution)/shard_map/ppermute | solution.py:367
  221.2 4.4 %collective-permute-start.11 = (bf16[8,4096]{1,0:T(8,128)(2,1)S(1)}, bf16[8,4096]{1,0:T(8,128)(2,1)S(1)}, u32[]{:S(2)}, u32[]{:S(2)}) collective-permute-start(bf16[8,4096]{1,0:T(8,128)(2,1)S(1)} %add_convert_fusion), channel_id=1, source_target_pairs={{0,32},{32,64},{64,96},{96,128},{128,160},{160,192},{192,224},{224... | collective-permute-start | bytes 196616 | tf_op jit(solution)/shard_map/ppermute | solution.py:388
  226.5 15.0 %all-to-all-start.8 = ((f32[32,8,128]{2,1,0:T(8,128)}), f32[32,8,128]{2,1,0:T(8,128)S(1)}, u32[]{:S(2)}, u32[]{:S(2)}) async-start(f32[32,8,128]{2,1,0:T(8,128)} %broadcast_in_dim.18), calls=%async_computation.8 | async-start | bytes 262144 | tf_op jit(solution)/shard_map/all_to_all | solution.py:399

commit v3 on v2

--- a/solution.py
+++ b/solution.py
@@ -14,6 +14,7 @@
 
 
 MIB = 1024 * 1024
+STAGGER = 1200
 RING = tuple(
     4 * x + y
     for x, y in ((0, 0), (0, 1), (0, 2), (0, 3), (1, 3), (1, 2), (1, 1), (2, 1))
@@ -232,6 +233,12 @@
 
     send_block(mixed, factor, downs, part_ref)
 
+    if iteration < ITERS - 1:
+
+        @pl.when(lax.axis_index("dp") % 2 == 1)
+        def _():
+            mix_ref[7:8] = lax.fori_loop(0, STAGGER, lambda _, v: v * 0.5 + 0.5, mix_ref[7:8])
+
 
 def folded_lanes(values):
     pieces = [values[:, n : n + 128] for n in range(0, values.shape[1], 128)]
@@ -310,13 +317,6 @@
     same_core = [[2 * h + c for h in order] for c in range(2)]
     across = [(d, d ^ 1) for d in range(groups)]
     ahead = [(s, (s + 1) % sections) for s in range(sections)]
-    ahead_across = [
-        (s * groups + d, (s + 1) % sections * groups + (d ^ 1))
-        for s in range(sections)
-        for d in range(groups)
-    ]
-    both = ("section", "dp")
-
     def to_chips(array):
         return lax.all_to_all(array, "dp", 0, 0, tiled=True, axis_index_groups=same_core)
 
@@ -329,9 +329,9 @@
     mine_w = [w_gate[0].T, w_up[0].T, w_down[0]]
     part0 = pallas(start_body, shape((8, features // 8), BF16), "start", 12)(gain, *mine_w)
     other_w = [lax.ppermute(w, "dp", across) for w in mine_w]
-    near = lax.ppermute(part0, "section", ahead)
-    far = lax.ppermute(part0, both, ahead_across)
-    start_part = (near.astype(F32) + far.astype(F32)).astype(BF16)
+    other0 = lax.ppermute(part0, "dp", across)
+    pair0 = (part0.astype(F32) + other0.astype(F32)).astype(BF16)
+    start_part = lax.ppermute(pair0, "section", ahead)
     first = to_all(jnp.concatenate([mine, start_part], axis=1))
 
     part_shape = shape((tokens, features), BF16)

time: 244 us -> 245 us (level)
  Pallas kernels: 31.6 us -> 44.2 us
  starting transfers between devices: 29.2 us -> 17.5 us
  waiting for transfers between devices: 28.6 us -> 34 us
  blocking collectives: 145 us -> 140 us
    pallas_call x3, Pallas kernels: 9.42 us -> 22 us  [local(): pallas(body, shapes, f'block{iteration}', 12, held)]
    ppermute x3, starting transfers between devices: 16.1 us -> 5.7 us  [local(): other_row = lax.ppermute(row, 'dp', across)]
    all_to_all x8, blocking collectives: 145 us -> 140 us  [to_chips(): lax.all_to_all(array, 'dp', 0, 0, tiled=True, axis_index_groups=same_core)]
    ppermute x2, waiting for transfers between devices: 3.65 us -> 9.06 us  [the longest x1 4.9 us: local(): start_part = lax.ppermute(pair0, 'section', ahead)]
  transfers between devices with their start and end apart: 13 -> 13, of which waited for: 6 -> 7; matrix products, arithmetic and copies ran while one was open for 0% -> 0% of each run, Pallas kernels for 5% -> 5%
where the time goes in v3:
time: 245 us
  blocking collectives  140 us (57%)
  Pallas kernels  44.2 us (18%)
  waiting for transfers between devices  34 us (14%)
  starting transfers between devices  17.5 us (7%)
  local copies, waits for them, and re-layouts  7.76 us (3%)
    all_to_all x8, blocking collectives, to_chips(): lax.all_to_all(array, 'dp', 0, 0, tiled=True, axis_index_groups=same_core)  140 us
    pallas_call x3, Pallas kernels, local(): pallas(body, shapes, f'block{iteration}', 12, held)  22 us
    ppermute x4, waiting for transfers between devices, local(): before = lax.ppermute((own_xs[-1] + total).astype(BF16), 'section', ahead)  17.3 us
    pallas_call x3, Pallas kernels, local(): pallas(products_body, pre_shape, f'products{iteration}', 12, cost=cost)  9.35 us
    all_to_all x1, waiting for transfers between devices, local(): lax.all_to_all(copies, 'dp', 0, 0, tiled=True).reshape(8 * groups, 128)  7.64 us
    all_to_all x1, starting transfers between devices, local(): lax.all_to_all(copies, 'dp', 0, 0, tiled=True).reshape(8 * groups, 128)  7.47 us
    unnamed x19, local copies, waits for them, and re-layouts  6.7 us
    ppermute x3, starting transfers between devices, local(): other_row = lax.ppermute(row, 'dp', across)  5.7 us
  transfers between devices with their start and end apart: 13, of which 7 were waited for; matrix products, arithmetic and copies ran while one was open for 0% of the time, Pallas kernels for 5%

profile of v3, /device:TPU:1, one launch (start us, length us, event | category | flops | bytes accessed | tf_op | source)
XLA Modules:
  0.0 244.7 jit_solution(3566932482496596792)
XLA Ops:
  0.6 3.3 %collective-permute-start.2 = (bf16[344,4096]{1,0:T(8,128)(2,1)}, bf16[344,4096]{1,0:T(8,128)(2,1)S(1)}, u32[]{:S(2)}, u32[]{:S(2)}) collective-permute-start(bf16[344,4096]{1,0:T(8,128)(2,1)} %bitcast.26), channel_id=1, source_target_pairs={{0,1},{1,0},{2,3},{3,2},{4,5},{5,4},{6,7},{7,6},{8,9},{9,8},{10,11... | collective-permute-start | bytes 8454152 | tf_op jit(solution)/shard_map/ppermute | solution.py:331
  3.9 0.1 collective-permute-start.3
  4.0 0.4 collective-permute-start.4
  4.4 1.8 copy-done
  6.2 1.8 copy-done.2
  8.0 1.8 copy-done.4
  9.8 0.7 copy-done.7
  10.5 2.1 start.1
  12.7 0.2 collective-permute-start
  12.9 4.2 %collective-permute-done = bf16[8,512]{1,0:T(8,128)(2,1)S(1)} collective-permute-done((bf16[8,512]{1,0:T(8,128)(2,1)S(1)}, bf16[8,512]{1,0:T(8,128)(2,1)S(1)}, u32[]{:S(2)}, u32[]{:S(2)}) %collective-permute-start) | collective-permute-done | bytes 8224 | tf_op jit(solution)/shard_map/ppermute | solution.py:332
  17.0 4.9 %collective-permute-done.1 = bf16[8,512]{1,0:T(8,128)(2,1)S(1)} collective-permute-done((bf16[8,512]{1,0:T(8,128)(2,1)S(1)}, bf16[8,512]{1,0:T(8,128)(2,1)S(1)}, u32[]{:S(2)}, u32[]{:S(2)}) %collective-permute-start.1) | collective-permute-done | bytes 8224 | tf_op jit(solution)/shard_map/ppermute | solution.py:334
  22.0 23.0 %all_to_all.45 = bf16[16,8,4608]{2,1,0:T(8,128)(2,1)S(1)} all-to-all(bf16[16,8,4608]{2,1,0:T(8,128)(2,1)S(1)} %broadcast_in_dim.14), channel_id=1, replica_groups={{0,2,4,6,14,12,10,18,20,22,30,28,26,24,16,8},{1,3,5,7,15,13,11,19,21,23..., dimensions={0} | all-to-all | bytes 2359296 | tf_op jit(solution)/shard_map/all_to_all | solution.py:321
  45.1 4.5 %block1.1 = (bf16[128,4096]{1,0:T(8,128)(2,1)S(1)}, f32[128,4096]{1,0:T(8,128)S(1)}, f32[8,4096]{1,0:T(8,128)S(1)}, f32[1376,128]{1,0:T(8,128)S(1)}) custom-call(bf16[128,4608]{1,0:T(8,128)(2,1)S(1)} %bitcast.19, f32[1,4096]{1,0:T(1,128)S(1)} %copy-done.8, bf16[344,4096]{1,0:T(8,128)(2,1)S(1)} %bitcast.28, bf16[344,4096]{1,0:T(8,128)(2,1)S(1)} %bitcast.34, ...), custom_call_target="tpu_custom_call" | custom-call | tf_op jit(solution)/shard_map/block1/pallas_call | solution.py:359
  49.5 16.1 %all_to_all.46 = bf16[16,8,4096]{2,1,0:T(8,128)(2,1)S(1)} all-to-all(bf16[16,8,4096]{2,1,0:T(8,128)(2,1)S(1)} %bitcast.56), channel_id=1, replica_groups={{0,2,4,6,14,12,10,18,20,22,30,28,26,24,16,8},{1,3,5,7,15,13,11,19,21,23..., dimensions={0} | all-to-all | bytes 2097152 | tf_op jit(solution)/shard_map/all_to_all | solution.py:321
  65.6 0.1 convert_reduce_fusion.3
  65.9 4.3 %collective-permute-done.5.refs_0_ = bf16[8,4096]{1,0:T(8,128)(2,1)S(1)} collective-permute-done((bf16[8,4096]{1,0:T(8,128)(2,1)S(1)}, bf16[8,4096]{1,0:T(8,128)(2,1)S(1)}, u32[]{:S(2)}, u32[]{:S(2)}) %collective-permute-start.5) | collective-permute-done | bytes 65568 | tf_op jit(solution)/shard_map/ppermute | solution.py:388
  70.2 0.1 broadcast_in_dim.15
  70.3 17.4 %all_to_all.47 = bf16[16,8,4096]{2,1,0:T(8,128)(2,1)S(1)} all-to-all(bf16[16,8,4096]{2,1,0:T(8,128)(2,1)S(1)} %broadcast_in_dim.15), channel_id=1, replica_groups={{0,2,4,6,14,12,10,18,20,22,30,28,26,24,16,8},{1,3,5,7,15,13,11,19,21,23..., dimensions={0} | all-to-all | bytes 2097152 | tf_op jit(solution)/shard_map/all_to_all | solution.py:321
  87.7 1.3 misfit1.1
  89.0 5.5 %collective-permute-start.6 = (f32[8,128]{1,0:T(8,128)S(1)}, f32[8,128]{1,0:T(8,128)S(1)}, u32[]{:S(2)}, u32[]{:S(2)}) collective-permute-start(f32[8,128]{1,0:T(8,128)S(1)} %get-tuple-element.33.refs_0_), channel_id=1, source_target_pairs={{0,1},{1,0},{2,3},{3,2},{4,5},{5,4},{6,7},{7,6},{8,9},{9,8},{10,11... | collective-permute-start | bytes 12296 | tf_op jit(solution)/shard_map/ppermute | solution.py:367
  94.5 3.1 %products2.1.refs_5_.refs_6_.refs_7_ = f32[1376,128]{1,0:T(8,128)S(1)} custom-call(bf16[128,4096]{1,0:T(8,128)(2,1)S(1)} %get-tuple-element.35.rows_ref, bf16[344,4096]{1,0:T(8,128)(2,1)S(1)} %bitcast.29, bf16[344,4096]{1,0:T(8,128)(2,1)S(1)} %bitcast.35, bf16[344,4096]{1,0:T(8,128)(2,1)S(1)} %collective-permute-done.2.refs_2_, ...), custom_call_target="tpu_custom_call" | custom-call | flops 1442840576 | bytes 11272192 | tf_op jit(solution)/shard_map/products2/pallas_call | solution.py:369
  97.7 8.9 %block2.1 = (bf16[128,4096]{1,0:T(8,128)(2,1)S(1)}, f32[8,4096]{1,0:T(8,128)S(1)}, f32[8,128]{1,0:T(8,128)S(1)}, f32[8,128]{1,0:T(8,128)S(1)}, f32[128,4096]{1,0:T(8,128)S(1)}) custom-call(f32[8,128]{1,0:T(8,128)S(1)} %get-tuple-element.33.refs_0_, f32[8,128]{1,0:T(8,128)S(1)} %collective-permute-done.6.refs_1_, bf16[128,4608]{1,0:T(8,128)(2,1)S(1)} %bitcast.21, ...), custom_call_target="tpu_custom_call" | custom-call | tf_op jit(solution)/shard_map/block2/pallas_call | solution.py:379
  106.5 14.6 %all_to_all.48 = bf16[16,8,4096]{2,1,0:T(8,128)(2,1)S(1)} all-to-all(bf16[16,8,4096]{2,1,0:T(8,128)(2,1)S(1)} %bitcast.55), channel_id=1, replica_groups={{0,2,4,6,14,12,10,18,20,22,30,28,26,24,16,8},{1,3,5,7,15,13,11,19,21,23..., dimensions={0} | all-to-all | bytes 2097152 | tf_op jit(solution)/shard_map/all_to_all | solution.py:321
  121.1 0.1 convert_reduce_fusion.2
  121.4 4.3 %collective-permute-done.7.refs_1_ = bf16[8,4096]{1,0:T(8,128)(2,1)S(1)} collective-permute-done((bf16[8,4096]{1,0:T(8,128)(2,1)S(1)}, bf16[8,4096]{1,0:T(8,128)(2,1)S(1)}, u32[]{:S(2)}, u32[]{:S(2)}) %collective-permute-start.7) | collective-permute-done | bytes 65568 | tf_op jit(solution)/shard_map/ppermute | solution.py:388
  125.7 0.1 broadcast_in_dim.16
  125.8 17.4 %all_to_all.49 = bf16[16,8,4096]{2,1,0:T(8,128)(2,1)S(1)} all-to-all(bf16[16,8,4096]{2,1,0:T(8,128)(2,1)S(1)} %broadcast_in_dim.16), channel_id=1, replica_groups={{0,2,4,6,14,12,10,18,20,22,30,28,26,24,16,8},{1,3,5,7,15,13,11,19,21,23..., dimensions={0} | all-to-all | bytes 2097152 | tf_op jit(solution)/shard_map/all_to_all | solution.py:321
  143.2 1.4 misfit2.1
  144.7 0.1 collective-permute-start.8
  144.8 3.1 %products3.1.refs_7_.refs_8_ = f32[1376,128]{1,0:T(8,128)S(1)} custom-call(bf16[128,4096]{1,0:T(8,128)(2,1)S(1)} %get-tuple-element.41.rows_ref, bf16[344,4096]{1,0:T(8,128)(2,1)S(1)} %bitcast.30, bf16[344,4096]{1,0:T(8,128)(2,1)S(1)} %bitcast.36, bf16[344,4096]{1,0:T(8,128)(2,1)S(1)} %collective-permute-done.2.refs_2_, ...), custom_call_target="tpu_custom_call" | custom-call | flops 1442840576 | bytes 11272192 | tf_op jit(solution)/shard_map/products3/pallas_call | solution.py:369
  147.9 9.4 %block3.1 = (bf16[128,4096]{1,0:T(8,128)(2,1)S(1)}, f32[8,4096]{1,0:T(8,128)S(1)}, f32[8,128]{1,0:T(8,128)S(1)}, f32[8,128]{1,0:T(8,128)S(1)}, f32[128,4096]{1,0:T(8,128)S(1)}) custom-call(f32[8,128]{1,0:T(8,128)S(1)} %get-tuple-element.40.refs_0_, f32[8,128]{1,0:T(8,128)S(1)} %collective-permute-done.8.refs_1_, bf16[128,4608]{1,0:T(8,128)(2,1)S(1)} %bitcast.23, ...), custom_call_target="tpu_custom_call" | custom-call | tf_op jit(solution)/shard_map/block3/pallas_call | solution.py:379
  157.3 15.2 %all_to_all.50 = bf16[16,8,4096]{2,1,0:T(8,128)(2,1)S(1)} all-to-all(bf16[16,8,4096]{2,1,0:T(8,128)(2,1)S(1)} %bitcast.54), channel_id=1, replica_groups={{0,2,4,6,14,12,10,18,20,22,30,28,26,24,16,8},{1,3,5,7,15,13,11,19,21,23..., dimensions={0} | all-to-all | bytes 2097152 | tf_op jit(solution)/shard_map/all_to_all | solution.py:321
  172.5 0.1 convert_reduce_fusion.1
  172.8 4.3 %collective-permute-done.9.refs_2_ = bf16[8,4096]{1,0:T(8,128)(2,1)S(1)} collective-permute-done((bf16[8,4096]{1,0:T(8,128)(2,1)S(1)}, bf16[8,4096]{1,0:T(8,128)(2,1)S(1)}, u32[]{:S(2)}, u32[]{:S(2)}) %collective-permute-start.9) | collective-permute-done | bytes 65568 | tf_op jit(solution)/shard_map/ppermute | solution.py:388
  177.1 0.1 broadcast_in_dim.17
  177.2 17.6 %all_to_all.51 = bf16[16,8,4096]{2,1,0:T(8,128)(2,1)S(1)} all-to-all(bf16[16,8,4096]{2,1,0:T(8,128)(2,1)S(1)} %broadcast_in_dim.17), channel_id=1, replica_groups={{0,2,4,6,14,12,10,18,20,22,30,28,26,24,16,8},{1,3,5,7,15,13,11,19,21,23..., dimensions={0} | all-to-all | bytes 2097152 | tf_op jit(solution)/shard_map/all_to_all | solution.py:321
  194.8 1.5 misfit3.1
  196.4 3.1 %products4.1.refs_9_ = f32[1376,128]{1,0:T(8,128)S(1)} custom-call(bf16[128,4096]{1,0:T(8,128)(2,1)S(1)} %get-tuple-element.48.rows_ref, bf16[344,4096]{1,0:T(8,128)(2,1)S(1)} %bitcast.31, bf16[344,4096]{1,0:T(8,128)(2,1)S(1)} %bitcast.37, bf16[344,4096]{1,0:T(8,128)(2,1)S(1)} %collective-permute-done.2.refs_2_, ...), custom_call_target="tpu_custom_call" | custom-call | flops 1442840576 | bytes 11272192 | tf_op jit(solution)/shard_map/products4/pallas_call | solution.py:369
  199.5 3.7 %block4.1 = (bf16[128,4096]{1,0:T(8,128)(2,1)S(1)}, f32[8,4096]{1,0:T(8,128)S(1)}, f32[8,128]{1,0:T(8,128)S(1)}, f32[8,128]{1,0:T(8,128)S(1)}) custom-call(f32[8,128]{1,0:T(8,128)S(1)} %get-tuple-element.47.refs_0_, f32[8,128]{1,0:T(8,128)S(1)} %collective-permute-done.10.refs_1_, bf16[128,4608]{1,0:T(8,128)(2,1)S(1)} %bitcast.25, ...), custom_call_target="tpu_custom_call" | custom-call | tf_op jit(solution)/shard_map/block4/pallas_call | solution.py:379
  203.3 18.4 %all_to_all.52 = bf16[16,8,4096]{2,1,0:T(8,128)(2,1)S(1)} all-to-all(bf16[16,8,4096]{2,1,0:T(8,128)(2,1)S(1)} %bitcast.53), channel_id=1, replica_groups={{0,2,4,6,14,12,10,18,20,22,30,28,26,24,16,8},{1,3,5,7,15,13,11,19,21,23..., dimensions={0} | all-to-all | bytes 2097152 | tf_op jit(solution)/shard_map/all_to_all | solution.py:321
  221.7 0.1 convert_reduce_fusion
  222.0 4.3 %collective-permute-done.11.refs_3_ = bf16[8,4096]{1,0:T(8,128)(2,1)S(1)} collective-permute-done((bf16[8,4096]{1,0:T(8,128)(2,1)S(1)}, bf16[8,4096]{1,0:T(8,128)(2,1)S(1)}, u32[]{:S(2)}, u32[]{:S(2)}) %collective-permute-start.11) | collective-permute-done | bytes 65568 | tf_op jit(solution)/shard_map/ppermute | solution.py:388
  226.3 0.2 last_misfit.1
  226.5 0.7 broadcast_in_dim.18
  227.2 7.5 %all-to-all-start.8 = ((f32[32,8,128]{2,1,0:T(8,128)}), f32[32,8,128]{2,1,0:T(8,128)S(1)}, u32[]{:S(2)}, u32[]{:S(2)}) async-start(f32[32,8,128]{2,1,0:T(8,128)} %broadcast_in_dim.18), calls=%async_computation.8 | async-start | bytes 262144 | tf_op jit(solution)/shard_map/all_to_all | solution.py:399
  234.7 7.6 %all-to-all-done.8 = f32[32,8,128]{2,1,0:T(8,128)S(1)} async-done(((f32[32,8,128]{2,1,0:T(8,128)}), f32[32,8,128]{2,1,0:T(8,128)S(1)}, u32[]{:S(2)}, u32[]{:S(2)}) %all-to-all-start.8) | async-done | bytes 131104 | tf_op jit(solution)/shard_map/all_to_all | solution.py:399
  242.3 1.7 final.1
  244.1 0.6 copy.7
  (38 shorter events, 0.7 us)
Async XLA Ops:
  0.6 44.4 %collective-permute-start.2 = (bf16[344,4096]{1,0:T(8,128)(2,1)}, bf16[344,4096]{1,0:T(8,128)(2,1)S(1)}, u32[]{:S(2)}, u32[]{:S(2)}) collective-permute-start(bf16[344,4096]{1,0:T(8,128)(2,1)} %bitcast.26), channel_id=1, source_target_pairs={{0,1},{1,0},{2,3},{3,2},{4,5},{5,4},{6,7},{7,6},{8,9},{9,8},{10,11... | collective-permute-start | bytes 8454152 | tf_op jit(solution)/shard_map/ppermute | solution.py:331
  3.9 41.1 %collective-permute-start.3 = (bf16[344,4096]{1,0:T(8,128)(2,1)}, bf16[344,4096]{1,0:T(8,128)(2,1)S(1)}, u32[]{:S(2)}, u32[]{:S(2)}) collective-permute-start(bf16[344,4096]{1,0:T(8,128)(2,1)} %bitcast.32), channel_id=1, source_target_pairs={{0,1},{1,0},{2,3},{3,2},{4,5},{5,4},{6,7},{7,6},{8,9},{9,8},{10,11... | collective-permute-start | bytes 8454152 | tf_op jit(solution)/shard_map/ppermute | solution.py:331
  4.0 41.0 %collective-permute-start.4 = (bf16[344,4096]{1,0:T(8,128)(2,1)}, bf16[344,4096]{1,0:T(8,128)(2,1)S(1)}, u32[]{:S(2)}, u32[]{:S(2)}) collective-permute-start(bf16[344,4096]{1,0:T(8,128)(2,1)} %bitcast.38), channel_id=1, source_target_pairs={{0,1},{1,0},{2,3},{3,2},{4,5},{5,4},{6,7},{7,6},{8,9},{9,8},{10,11... | collective-permute-start | bytes 8454152 | tf_op jit(solution)/shard_map/ppermute | solution.py:331
  4.4 1.8 copy-start
  6.2 1.8 copy-start.2
  8.0 1.8 copy-start.4
  9.8 0.7 copy-start.7
  10.5 11.4 %copy-start.6 = (bf16[1,8,4096]{2,1,0:T(8,128)(2,1)S(1)}, bf16[1,8,4096]{2,1,0:T(8,128)(2,1)}, u32[]{:S(2)}) copy-start(bf16[1,8,4096]{2,1,0:T(8,128)(2,1)} %param.5) | copy-start | bytes 196612
  10.5 34.5 %copy-start.3 = (bf16[1,4096,344]{1,2,0:T(8,128)(2,1)S(1)}, bf16[1,4096,344]{1,2,0:T(8,128)(2,1)}, u32[]{:S(2)}) copy-start(bf16[1,4096,344]{1,2,0:T(8,128)(2,1)} %param.7) | copy-start | bytes 8454148
  12.7 32.4 %copy-start.1 = (bf16[1,4096,344]{1,2,0:T(8,128)(2,1)S(1)}, bf16[1,4096,344]{1,2,0:T(8,128)(2,1)}, u32[]{:S(2)}) copy-start(bf16[1,4096,344]{1,2,0:T(8,128)(2,1)} %param.6) | copy-start | bytes 8454148
  12.7 32.4 %copy-start.8 = (f32[1,4096]{1,0:T(1,128)S(1)}, f32[1,4096]{1,0:T(1,128)}, u32[]{:S(2)}) copy-start(f32[1,4096]{1,0:T(1,128)} %gain_ref.9) | copy-start | bytes 49156
  12.7 4.3 %collective-permute-start = (bf16[8,512]{1,0:T(8,128)(2,1)S(1)}, bf16[8,512]{1,0:T(8,128)(2,1)S(1)}, u32[]{:S(2)}, u32[]{:S(2)}) collective-permute-start(bf16[8,512]{1,0:T(8,128)(2,1)S(1)} %start.1), channel_id=1, source_target_pairs={{0,1},{1,0},{2,3},{3,2},{4,5},{5,4},{6,7},{7,6},{8,9},{9,8},{10,11... | collective-permute-start | bytes 24584 | tf_op jit(solution)/shard_map/ppermute | solution.py:332
  17.0 4.9 %collective-permute-start.1 = (bf16[8,512]{1,0:T(8,128)(2,1)S(1)}, bf16[8,512]{1,0:T(8,128)(2,1)S(1)}, u32[]{:S(2)}, u32[]{:S(2)}) collective-permute-start(bf16[8,512]{1,0:T(8,128)(2,1)S(1)} %add_convert_fusion.4), channel_id=1, source_target_pairs={{0,32},{32,64},{64,96},{96,128},{128,160},{160,192},{192,224},{224... | collective-permute-start | bytes 24584 | tf_op jit(solution)/shard_map/ppermute | solution.py:334
  65.8 4.4 %collective-permute-start.5 = (bf16[8,4096]{1,0:T(8,128)(2,1)S(1)}, bf16[8,4096]{1,0:T(8,128)(2,1)S(1)}, u32[]{:S(2)}, u32[]{:S(2)}) collective-permute-start(bf16[8,4096]{1,0:T(8,128)(2,1)S(1)} %add_convert_fusion.3), channel_id=1, source_target_pairs={{0,32},{32,64},{64,96},{96,128},{128,160},{160,192},{192,224},{224... | collective-permute-start | bytes 196616 | tf_op jit(solution)/shard_map/ppermute | solution.py:388
  89.0 8.6 %collective-permute-start.6 = (f32[8,128]{1,0:T(8,128)S(1)}, f32[8,128]{1,0:T(8,128)S(1)}, u32[]{:S(2)}, u32[]{:S(2)}) collective-permute-start(f32[8,128]{1,0:T(8,128)S(1)} %get-tuple-element.33.refs_0_), channel_id=1, source_target_pairs={{0,1},{1,0},{2,3},{3,2},{4,5},{5,4},{6,7},{7,6},{8,9},{9,8},{10,11... | collective-permute-start | bytes 12296 | tf_op jit(solution)/shard_map/ppermute | solution.py:367
  94.5 3.1 %copy-start.5 = (bf16[1,344,4096]{2,1,0:T(8,128)(2,1)S(1)}, bf16[1,344,4096]{2,1,0:T(8,128)(2,1)}, u32[]{:S(2)}) copy-start(bf16[1,344,4096]{2,1,0:T(8,128)(2,1)} %param.8) | copy-start | bytes 8454148
  121.3 4.4 %collective-permute-start.7 = (bf16[8,4096]{1,0:T(8,128)(2,1)S(1)}, bf16[8,4096]{1,0:T(8,128)(2,1)S(1)}, u32[]{:S(2)}, u32[]{:S(2)}) collective-permute-start(bf16[8,4096]{1,0:T(8,128)(2,1)S(1)} %add_convert_fusion.2), channel_id=1, source_target_pairs={{0,32},{32,64},{64,96},{96,128},{128,160},{160,192},{192,224},{224... | collective-permute-start | bytes 196616 | tf_op jit(solution)/shard_map/ppermute | solution.py:388
  144.7 3.2 %collective-permute-start.8 = (f32[8,128]{1,0:T(8,128)S(1)}, f32[8,128]{1,0:T(8,128)S(1)}, u32[]{:S(2)}, u32[]{:S(2)}) collective-permute-start(f32[8,128]{1,0:T(8,128)S(1)} %get-tuple-element.40.refs_0_), channel_id=1, source_target_pairs={{0,1},{1,0},{2,3},{3,2},{4,5},{5,4},{6,7},{7,6},{8,9},{9,8},{10,11... | collective-permute-start | bytes 12296 | tf_op jit(solution)/shard_map/ppermute | solution.py:367
  172.7 4.4 %collective-permute-start.9 = (bf16[8,4096]{1,0:T(8,128)(2,1)S(1)}, bf16[8,4096]{1,0:T(8,128)(2,1)S(1)}, u32[]{:S(2)}, u32[]{:S(2)}) collective-permute-start(bf16[8,4096]{1,0:T(8,128)(2,1)S(1)} %add_convert_fusion.1), channel_id=1, source_target_pairs={{0,32},{32,64},{64,96},{96,128},{128,160},{160,192},{192,224},{224... | collective-permute-start | bytes 196616 | tf_op jit(solution)/shard_map/ppermute | solution.py:388
  196.3 3.2 %collective-permute-start.10 = (f32[8,128]{1,0:T(8,128)S(1)}, f32[8,128]{1,0:T(8,128)S(1)}, u32[]{:S(2)}, u32[]{:S(2)}) collective-permute-start(f32[8,128]{1,0:T(8,128)S(1)} %get-tuple-element.47.refs_0_), channel_id=1, source_target_pairs={{0,1},{1,0},{2,3},{3,2},{4,5},{5,4},{6,7},{7,6},{8,9},{9,8},{10,11... | collective-permute-start | bytes 12296 | tf_op jit(solution)/shard_map/ppermute | solution.py:367
  221.9 4.4 %collective-permute-start.11 = (bf16[8,4096]{1,0:T(8,128)(2,1)S(1)}, bf16[8,4096]{1,0:T(8,128)(2,1)S(1)}, u32[]{:S(2)}, u32[]{:S(2)}) collective-permute-start(bf16[8,4096]{1,0:T(8,128)(2,1)S(1)} %add_convert_fusion), channel_id=1, source_target_pairs={{0,32},{32,64},{64,96},{96,128},{128,160},{160,192},{192,224},{224... | collective-permute-start | bytes 196616 | tf_op jit(solution)/shard_map/ppermute | solution.py:388
  227.2 15.1 %all-to-all-start.8 = ((f32[32,8,128]{2,1,0:T(8,128)}), f32[32,8,128]{2,1,0:T(8,128)S(1)}, u32[]{:S(2)}, u32[]{:S(2)}) async-start(f32[32,8,128]{2,1,0:T(8,128)} %broadcast_in_dim.18), calls=%async_computation.8 | async-start | bytes 262144 | tf_op jit(solution)/shard_map/all_to_all | solution.py:399

commit v4 on v2

--- a/solution.py
+++ b/solution.py
@@ -138,8 +138,14 @@
         pre_ref[i * hidden : (i + 1) * hidden] = by_rows(w_ref[...], rows_ref[...])
 
 
+def on_core(core):
+    return pl.when(lax.axis_index("dp") % 2 == core)
+
+
 def products_body(rows_ref, *refs):
-    products(rows_ref, refs[:4], refs[4])
+    @on_core(1)
+    def _():
+        products(rows_ref, refs[:4], refs[4])
 
 
 def lane_rsqrt(squares_ref, features):
@@ -195,18 +201,28 @@
 def block_body(iteration, cells, order, *refs):
     own_ref, other_ref, first_ref = refs[:3]
     outs = refs[3 : 2 + iteration]
-    pres = refs[2 + iteration : 2 + 2 * iteration]
+    ready_ref = refs[2 + iteration]
+    pres = refs[3 + iteration : 2 + 2 * iteration]
     at = 2 + 2 * iteration
     state = None
     if iteration > 2:
         state = refs[at][...]
         at += 1
-    downs = refs[at : at + 2]
-    if iteration < ITERS - 1:
-        part_ref, own_x_ref, kept_ref, mix_ref, x_ref, squares_ref = refs[at + 2 :]
-    else:
-        part_ref, own_x_ref, kept_ref, mix_ref, squares_ref, x_ref = refs[at + 2 :]
+    scaled_ref, weights, downs = refs[at], refs[at + 1 : at + 5], refs[at + 5 : at + 7]
+    part_ref, own_x_ref, kept_ref, mix_ref, *rest = refs[at + 7 :]
+    squares_ref = rest[-1]
+    x_ref, pre_ref = rest[:2]
     tokens, features = part_ref.shape
+
+    @on_core(0)
+    def _():
+        products(scaled_ref, weights, pre_ref)
+
+    @on_core(1)
+    def _():
+        pre_ref[...] = ready_ref[...]
+
+    pres = (*pres, pre_ref)
     fresh = own_ref[...] + other_ref[...]
     kept, mix, entries = gram_and_weights(fresh, state, iteration - 1, cells)
     kept_ref[...] = kept
@@ -215,12 +231,17 @@
     for i in range(1, iteration):
         total = total + mix[i]
     base = (0.5 * mix[0]) * start_row(first_ref, features)
-    for h in range(0, tokens, 16):
-        rows = total * first_ref[h : h + 16, :features].astype(F32) + base
+
+    def step(h, _):
+        at = pl.ds(pl.multiple_of(16 * h, 16), 16)
+        rows = total * first_ref[at, :features].astype(F32) + base
         for i in range(1, iteration):
-            rows = rows + (0.5 * mix[i]) * outs[i - 1][h : h + 16, :].astype(F32)
-        x_ref[h : h + 16, :] = rows
-        squares_ref[h : h + 16, :] = squares_of(rows)
+            rows = rows + (0.5 * mix[i]) * outs[i - 1][at, :].astype(F32)
+        x_ref[at, :] = rows
+        squares_ref[at, :] = squares_of(rows)
+        return 0
+
+    lax.fori_loop(0, tokens // 16, step, 0)
     own_x_ref[...] = own_rows(x_ref, order)
     factor = lane_rsqrt(squares_ref, features)
 
@@ -256,23 +277,24 @@
     befores = refs[:iteration]
     row_ref, scaled_ref, *kept = refs[iteration:]
     tokens, features = x_ref.shape
-    sums = [jnp.zeros((8, 128), F32) for _ in range(iteration + 1)]
-    first = jnp.zeros((8, 128), F32)
-    for h in range(0, tokens, 16):
-        at = slice(h, h + 16)
+
+    def step(h, sums):
+        at = pl.ds(pl.multiple_of(16 * h, 16), 16)
         image = first_ref[at, :features].astype(F32) + 0.5 * out_ref[at, :].astype(F32)
         scaled_ref[at, :] = (image * gain_ref[...]).astype(BF16)
         misfit = image - x_ref[at, :]
         if kept:
             kept[0][at, :] = misfit
-        for j in range(iteration + 1):
-            other = misfit if j == iteration else befores[j][at, :]
-            prod = folded_lanes(misfit * other)
-            sums[j] = sums[j] + prod[:8] + prod[8:]
+        pairs = [(misfit, befores[j][at, :]) for j in range(iteration)] + [(misfit, misfit)]
         if iteration == 1:
-            prod = folded_lanes(befores[0][at, :] * befores[0][at, :])
-            first = first + prod[:8] + prod[8:]
-    row_ref[...] = gram_row(sums, first if iteration == 1 else None)
+            pairs.append((befores[0][at, :], befores[0][at, :]))
+        prods = [folded_lanes(a * b) for a, b in pairs]
+        return tuple(s + p[:8] + p[8:] for s, p in zip(sums, prods))
+
+    count = iteration + 1 + (iteration == 1)
+    zero = tuple(jnp.zeros((8, 128), F32) for _ in range(count))
+    sums = lax.fori_loop(0, tokens // 16, step, zero)
+    row_ref[...] = gram_row(sums[: iteration + 1], sums[-1] if iteration == 1 else None)
 
 
 def last_misfit_body(inject_ref, *refs):
@@ -281,7 +303,9 @@
     misfits = [xs[0][...]]
     for out_ref, x_ref in zip(outs, xs):
         misfits.append(inject + 0.5 * out_ref[...].astype(F32) - x_ref[...])
-    row_ref[...] = gram_row([folded_lanes(misfits[-1] * m) for m in misfits], None)
+    row = gram_row([folded_lanes(misfits[-1] * m) for m in misfits], None)
+    for d in range(0, row_ref.shape[0], 8):
+        row_ref[d : d + 8] = row
 
 
 def final_body(cells, rows_ref, inject_ref, start_ref, state_ref, *refs):
@@ -315,7 +339,6 @@
         for s in range(sections)
         for d in range(groups)
     ]
-    both = ("section", "dp")
 
     def to_chips(array):
         return lax.all_to_all(array, "dp", 0, 0, tiled=True, axis_index_groups=same_core)
@@ -330,7 +353,7 @@
     part0 = pallas(start_body, shape((8, features // 8), BF16), "start", 12)(gain, *mine_w)
     other_w = [lax.ppermute(w, "dp", across) for w in mine_w]
     near = lax.ppermute(part0, "section", ahead)
-    far = lax.ppermute(part0, both, ahead_across)
+    far = lax.ppermute(part0, ("section", "dp"), ahead_across)
     start_part = (near.astype(F32) + far.astype(F32)).astype(BF16)
     first = to_all(jnp.concatenate([mine, start_part], axis=1))
 
@@ -364,22 +387,22 @@
         else:
             body = functools.partial(block_body, iteration, cells, order)
             carried = [] if state is None else [state]
+            ready = pallas(products_body, pre_shape, f"products{iteration}", 12, cost=cost)(
+                scaled, *weights
+            )
+            row, ready = lax.optimization_barrier((row, ready))
             other_row = lax.ppermute(row, "dp", across)
-            pres.append(
-                pallas(products_body, pre_shape, f"products{iteration}", 12, cost=cost)(
-                    scaled, *weights
-                )
-            )
             shapes = [part_shape, own_shape, small, small]
             held = [squares]
             if iteration < ITERS - 1:
-                shapes.append(wide_shape)
+                shapes += [wide_shape, pre_shape]
             else:
-                held.append(pltpu.VMEM((tokens, features), F32))
+                held = [pltpu.VMEM((tokens, features), F32), pltpu.VMEM(pre_shape.shape, F32), squares]
             part, own_x, state, mix, *rest = pallas(body, shapes, f"block{iteration}", 12, held)(
-                row, other_row, first, *gathered, *pres, *carried, *downs
+                row, other_row, first, *gathered, ready, *pres, *carried, scaled, *weights, *downs
             )
-            x = rest[0] if rest else None
+            x, pre = rest if rest else (None, None)
+            pres.append(pre)
             if iteration == 2:
                 mixing.append(mix[1, :HIST])
             mixing.append(mix[0, :HIST])
@@ -394,9 +417,9 @@
                 functools.partial(misfit_body, iteration), shapes, f"misfit{iteration}", 12
             )(first, gathered[-1], x, gain, *misfits)
             misfits += misfit
-    row = pallas(last_misfit_body, small, "last_misfit", 8)(mine, *own_outs, *own_xs)
-    copies = jnp.broadcast_to(row[None], (groups, *row.shape))
-    sums = lax.all_to_all(copies, "dp", 0, 0, tiled=True).reshape(8 * groups, 128)
+    copies = shape((8 * groups, 128), F32)
+    sums = pallas(last_misfit_body, copies, "last_misfit", 8)(mine, *own_outs, *own_xs)
+    sums = lax.all_to_all(sums, "dp", 0, 0, tiled=True)
     iterate, mix = pallas(functools.partial(final_body, cells), (own_shape, small), "final", 8)(
         sums, mine, own_xs[0], state, *own_outs
     )

time: 244 us -> 236 us (0.967)
  blocking collectives: 145 us -> 138 us
  starting transfers between devices: 29.2 us -> 23.8 us
  waiting for transfers between devices: 28.6 us -> 31.6 us
  Pallas kernels: 31.6 us -> 34.2 us
    ppermute x3, starting transfers between devices: 16.1 us -> 7.97 us  [local(): other_row = lax.ppermute(row, 'dp', across)]
    all_to_all x8, blocking collectives: 145 us -> 138 us  [to_chips(): lax.all_to_all(array, 'dp', 0, 0, tiled=True, axis_index_groups=same_core)]
    pallas_call x3, Pallas kernels: 9.42 us -> 12.2 us  [local(): pallas(body, shapes, f'block{iteration}', 12, held)]
    all_to_all x1, starting transfers between devices: 7.34 us -> 10.1 us  [local(): sums = lax.all_to_all(sums, 'dp', 0, 0, tiled=True)]
    ppermute x3, waiting for transfers between devices: 0.01 us -> 2.47 us  [local(): other_row = lax.ppermute(row, 'dp', across)]
  transfers between devices with their start and end apart: 13 -> 13, of which waited for: 6 -> 9; matrix products, arithmetic and copies ran while one was open for 0% -> 0% of each run, Pallas kernels for 5% -> 1%
where the time goes in v4:
time: 236 us
  blocking collectives  138 us (58%)
  Pallas kernels  34.2 us (14%)
  waiting for transfers between devices  31.6 us (13%)
  starting transfers between devices  23.8 us (10%)
  local copies, waits for them, and re-layouts  7.1 us (3%)
    all_to_all x8, blocking collectives, to_chips(): lax.all_to_all(array, 'dp', 0, 0, tiled=True, axis_index_groups=same_core)  138 us
    ppermute x4, waiting for transfers between devices, local(): before = lax.ppermute((own_xs[-1] + total).astype(BF16), 'section', ahead)  17.8 us
    pallas_call x3, Pallas kernels, local(): pallas(body, shapes, f'block{iteration}', 12, held)  12.2 us
    all_to_all x1, starting transfers between devices, local(): sums = lax.all_to_all(sums, 'dp', 0, 0, tiled=True)  10.1 us
    pallas_call x3, Pallas kernels, local(): pallas(products_body, pre_shape, f'products{iteration}', 12, cost=cost)  9.42 us
    ppermute x3, starting transfers between devices, local(): other_row = lax.ppermute(row, 'dp', across)  7.97 us
    all_to_all x1, waiting for transfers between devices, local(): sums = lax.all_to_all(sums, 'dp', 0, 0, tiled=True)  7.64 us
    unnamed x19, local copies, waits for them, and re-layouts  6.7 us
  transfers between devices with their start and end apart: 13, of which 9 were waited for; matrix products, arithmetic and copies ran while one was open for 0% of the time, Pallas kernels for 1%

profile of v4, /device:TPU:1, one launch (start us, length us, event | category | flops | bytes accessed | tf_op | source)
XLA Modules:
  0.0 235.9 jit_solution(7757656232873441496)
XLA Ops:
  0.6 3.3 %collective-permute-start.2 = (bf16[344,4096]{1,0:T(8,128)(2,1)}, bf16[344,4096]{1,0:T(8,128)(2,1)S(1)}, u32[]{:S(2)}, u32[]{:S(2)}) collective-permute-start(bf16[344,4096]{1,0:T(8,128)(2,1)} %bitcast.20), channel_id=1, source_target_pairs={{0,1},{1,0},{2,3},{3,2},{4,5},{5,4},{6,7},{7,6},{8,9},{9,8},{10,11... | collective-permute-start | bytes 8454152 | tf_op jit(solution)/shard_map/ppermute | solution.py:354
  3.9 0.1 collective-permute-start.3
  4.0 0.4 collective-permute-start.4
  4.4 1.8 copy-done
  6.2 1.8 copy-done.2
  8.0 1.8 copy-done.4
  9.8 0.7 copy-done.7
  10.5 2.1 start.1
  12.8 1.5 collective-permute-start
  14.3 3.7 %collective-permute-done.1 = bf16[8,512]{1,0:T(8,128)(2,1)S(1)} collective-permute-done((bf16[8,512]{1,0:T(8,128)(2,1)S(1)}, bf16[8,512]{1,0:T(8,128)(2,1)S(1)}, u32[]{:S(2)}, u32[]{:S(2)}) %collective-permute-start.1) | collective-permute-done | bytes 8224 | tf_op jit(solution)/shard_map/ppermute | solution.py:356
  18.1 23.9 %all_to_all.51 = bf16[16,8,4608]{2,1,0:T(8,128)(2,1)S(1)} all-to-all(bf16[16,8,4608]{2,1,0:T(8,128)(2,1)S(1)} %broadcast_in_dim.12), channel_id=1, replica_groups={{0,2,4,6,14,12,10,18,20,22,30,28,26,24,16,8},{1,3,5,7,15,13,11,19,21,23..., dimensions={0} | all-to-all | bytes 2359296 | tf_op jit(solution)/shard_map/all_to_all | solution.py:344
  42.0 4.5 %block1.1 = (bf16[128,4096]{1,0:T(8,128)(2,1)S(1)}, f32[128,4096]{1,0:T(8,128)S(1)}, f32[8,4096]{1,0:T(8,128)S(1)}, f32[1376,128]{1,0:T(8,128)S(1)}) custom-call(bf16[128,4608]{1,0:T(8,128)(2,1)S(1)} %bitcast.38, f32[1,4096]{1,0:T(1,128)S(1)} %copy-done.8, bf16[344,4096]{1,0:T(8,128)(2,1)S(1)} %bitcast.22, bf16[344,4096]{1,0:T(8,128)(2,1)S(1)} %bitcast.31, ...), custom_call_target="tpu_custom_call" | custom-call | tf_op jit(solution)/shard_map/block1/pallas_call | solution.py:382
  46.5 17.0 %all_to_all.52 = bf16[16,8,4096]{2,1,0:T(8,128)(2,1)S(1)} all-to-all(bf16[16,8,4096]{2,1,0:T(8,128)(2,1)S(1)} %bitcast.63), channel_id=1, replica_groups={{0,2,4,6,14,12,10,18,20,22,30,28,26,24,16,8},{1,3,5,7,15,13,11,19,21,23..., dimensions={0} | all-to-all | bytes 2097152 | tf_op jit(solution)/shard_map/all_to_all | solution.py:344
  63.5 0.1 convert_reduce_fusion.3
  63.8 4.3 %collective-permute-done.5.refs_0_ = bf16[8,4096]{1,0:T(8,128)(2,1)S(1)} collective-permute-done((bf16[8,4096]{1,0:T(8,128)(2,1)S(1)}, bf16[8,4096]{1,0:T(8,128)(2,1)S(1)}, u32[]{:S(2)}, u32[]{:S(2)}) %collective-permute-start.5) | collective-permute-done | bytes 65568 | tf_op jit(solution)/shard_map/ppermute | solution.py:411
  68.1 0.1 broadcast_in_dim.13
  68.2 15.2 %all_to_all.53 = bf16[16,8,4096]{2,1,0:T(8,128)(2,1)S(1)} all-to-all(bf16[16,8,4096]{2,1,0:T(8,128)(2,1)S(1)} %broadcast_in_dim.13), channel_id=1, replica_groups={{0,2,4,6,14,12,10,18,20,22,30,28,26,24,16,8},{1,3,5,7,15,13,11,19,21,23..., dimensions={0} | all-to-all | bytes 2097152 | tf_op jit(solution)/shard_map/all_to_all | solution.py:344
  83.4 1.0 misfit1.1
  84.4 3.1 %products2.1.refs_4_ = f32[1376,128]{1,0:T(8,128)S(1)} custom-call(bf16[128,4096]{1,0:T(8,128)(2,1)S(1)} %get-tuple-element.42.rows_ref.refs_6_, bf16[344,4096]{1,0:T(8,128)(2,1)S(1)} %bitcast.23, bf16[344,4096]{1,0:T(8,128)(2,1)S(1)} %bitcast.32, bf16[344,4096]{1,0:T(8,128)(2,1)S(1)} %collective-permute-done.2.refs_2_.refs_9_.refs_12_.refs_14_, ...), custom_call_target="tpu_custom_call" | custom-call | flops 1442840576 | bytes 11272192 | tf_op jit(solution)/shard_map/products2/pallas_call | solution.py:390
  87.6 3.0 %collective-permute-start.6 = (f32[8,128]{1,0:T(8,128)S(1)}, f32[8,128]{1,0:T(8,128)S(1)}, u32[]{:S(2)}, u32[]{:S(2)}) collective-permute-start(f32[8,128]{1,0:T(8,128)S(1)} %get-tuple-element.43.refs_0_), channel_id=1, source_target_pairs={{0,1},{1,0},{2,3},{3,2},{4,5},{5,4},{6,7},{7,6},{8,9},{9,8},{10,11... | collective-permute-start | bytes 12296 | tf_op jit(solution)/shard_map/ppermute | solution.py:394
  90.6 0.8 collective-permute-done.6.refs_1_
  91.4 3.5 %block2.1 = (bf16[128,4096]{1,0:T(8,128)(2,1)S(1)}, f32[8,4096]{1,0:T(8,128)S(1)}, f32[8,128]{1,0:T(8,128)S(1)}, f32[8,128]{1,0:T(8,128)S(1)}, f32[128,4096]{1,0:T(8,128)S(1)}, /*index=5*/f32[1376,128]{1,0:T(8,128)S(1)}) custom-call(f32[8,128]{1,0:T(8,128)S(1)} %get-tuple-element.43.refs_0_, f32[8,128]{1,0:T(8,128)S(1)} %collective-permute-done.6.refs_1_, ...), custom_call_target="tpu_custom_call" | custom-call | tf_op jit(solution)/shard_map/block2/pallas_call | solution.py:401
  94.9 15.5 %all_to_all.54 = bf16[16,8,4096]{2,1,0:T(8,128)(2,1)S(1)} all-to-all(bf16[16,8,4096]{2,1,0:T(8,128)(2,1)S(1)} %bitcast.62), channel_id=1, replica_groups={{0,2,4,6,14,12,10,18,20,22,30,28,26,24,16,8},{1,3,5,7,15,13,11,19,21,23..., dimensions={0} | all-to-all | bytes 2097152 | tf_op jit(solution)/shard_map/all_to_all | solution.py:344
  110.4 0.1 convert_reduce_fusion.2
  110.6 4.6 %collective-permute-done.7.refs_1_ = bf16[8,4096]{1,0:T(8,128)(2,1)S(1)} collective-permute-done((bf16[8,4096]{1,0:T(8,128)(2,1)S(1)}, bf16[8,4096]{1,0:T(8,128)(2,1)S(1)}, u32[]{:S(2)}, u32[]{:S(2)}) %collective-permute-start.7) | collective-permute-done | bytes 65568 | tf_op jit(solution)/shard_map/ppermute | solution.py:411
  115.4 16.8 %all_to_all.55 = bf16[16,8,4096]{2,1,0:T(8,128)(2,1)S(1)} all-to-all(bf16[16,8,4096]{2,1,0:T(8,128)(2,1)S(1)} %broadcast_in_dim.14), channel_id=1, replica_groups={{0,2,4,6,14,12,10,18,20,22,30,28,26,24,16,8},{1,3,5,7,15,13,11,19,21,23..., dimensions={0} | all-to-all | bytes 2097152 | tf_op jit(solution)/shard_map/all_to_all | solution.py:344
  132.2 1.1 misfit2.1
  133.3 3.1 %products3.1.refs_5_ = f32[1376,128]{1,0:T(8,128)S(1)} custom-call(bf16[128,4096]{1,0:T(8,128)(2,1)S(1)} %get-tuple-element.51.rows_ref.refs_9_, bf16[344,4096]{1,0:T(8,128)(2,1)S(1)} %bitcast.25, bf16[344,4096]{1,0:T(8,128)(2,1)S(1)} %bitcast.34, bf16[344,4096]{1,0:T(8,128)(2,1)S(1)} %collective-permute-done.2.refs_2_.refs_9_.refs_12_.refs_14_, ...), custom_call_target="tpu_custom_call" | custom-call | flops 1442840576 | bytes 11272192 | tf_op jit(solution)/shard_map/products3/pallas_call | solution.py:390
  136.4 2.8 %collective-permute-start.8 = (f32[8,128]{1,0:T(8,128)S(1)}, f32[8,128]{1,0:T(8,128)S(1)}, u32[]{:S(2)}, u32[]{:S(2)}) collective-permute-start(f32[8,128]{1,0:T(8,128)S(1)} %get-tuple-element.52.refs_0_), channel_id=1, source_target_pairs={{0,1},{1,0},{2,3},{3,2},{4,5},{5,4},{6,7},{7,6},{8,9},{9,8},{10,11... | collective-permute-start | bytes 12296 | tf_op jit(solution)/shard_map/ppermute | solution.py:394
  139.2 0.8 collective-permute-done.8.refs_1_
  140.0 4.0 %block3.1 = (bf16[128,4096]{1,0:T(8,128)(2,1)S(1)}, f32[8,4096]{1,0:T(8,128)S(1)}, f32[8,128]{1,0:T(8,128)S(1)}, f32[8,128]{1,0:T(8,128)S(1)}, f32[128,4096]{1,0:T(8,128)S(1)}, /*index=5*/f32[1376,128]{1,0:T(8,128)S(1)}) custom-call(f32[8,128]{1,0:T(8,128)S(1)} %get-tuple-element.52.refs_0_, f32[8,128]{1,0:T(8,128)S(1)} %collective-permute-done.8.refs_1_, ...), custom_call_target="tpu_custom_call" | custom-call | tf_op jit(solution)/shard_map/block3/pallas_call | solution.py:401
  144.1 15.8 %all_to_all.56 = bf16[16,8,4096]{2,1,0:T(8,128)(2,1)S(1)} all-to-all(bf16[16,8,4096]{2,1,0:T(8,128)(2,1)S(1)} %bitcast.61), channel_id=1, replica_groups={{0,2,4,6,14,12,10,18,20,22,30,28,26,24,16,8},{1,3,5,7,15,13,11,19,21,23..., dimensions={0} | all-to-all | bytes 2097152 | tf_op jit(solution)/shard_map/all_to_all | solution.py:344
  159.9 0.1 convert_reduce_fusion.1
  160.1 4.4 %collective-permute-done.9.refs_2_ = bf16[8,4096]{1,0:T(8,128)(2,1)S(1)} collective-permute-done((bf16[8,4096]{1,0:T(8,128)(2,1)S(1)}, bf16[8,4096]{1,0:T(8,128)(2,1)S(1)}, u32[]{:S(2)}, u32[]{:S(2)}) %collective-permute-start.9) | collective-permute-done | bytes 65568 | tf_op jit(solution)/shard_map/ppermute | solution.py:411
  164.6 17.8 %all_to_all.57 = bf16[16,8,4096]{2,1,0:T(8,128)(2,1)S(1)} all-to-all(bf16[16,8,4096]{2,1,0:T(8,128)(2,1)S(1)} %broadcast_in_dim.15), channel_id=1, replica_groups={{0,2,4,6,14,12,10,18,20,22,30,28,26,24,16,8},{1,3,5,7,15,13,11,19,21,23..., dimensions={0} | all-to-all | bytes 2097152 | tf_op jit(solution)/shard_map/all_to_all | solution.py:344
  182.4 1.2 misfit3.1
  183.7 3.1 %products4.1.refs_6_ = f32[1376,128]{1,0:T(8,128)S(1)} custom-call(bf16[128,4096]{1,0:T(8,128)(2,1)S(1)} %get-tuple-element.61.rows_ref.refs_11_, bf16[344,4096]{1,0:T(8,128)(2,1)S(1)} %bitcast.27, bf16[344,4096]{1,0:T(8,128)(2,1)S(1)} %bitcast.36, bf16[344,4096]{1,0:T(8,128)(2,1)S(1)} %collective-permute-done.2.refs_2_.refs_9_.refs_12_.refs_14_, ...), custom_call_target="tpu_custom_call" | custom-call | flops 1442840576 | bytes 11272192 | tf_op jit(solution)/shard_map/products4/pallas_call | solution.py:390
  186.8 2.2 collective-permute-start.10
  189.0 0.8 collective-permute-done.10.refs_1_
  189.8 4.7 %block4.1 = (bf16[128,4096]{1,0:T(8,128)(2,1)S(1)}, f32[8,4096]{1,0:T(8,128)S(1)}, f32[8,128]{1,0:T(8,128)S(1)}, f32[8,128]{1,0:T(8,128)S(1)}) custom-call(f32[8,128]{1,0:T(8,128)S(1)} %get-tuple-element.62.refs_0_, f32[8,128]{1,0:T(8,128)S(1)} %collective-permute-done.10.refs_1_, bf16[128,4608]{1,0:T(8,128)(2,1)S(1)} %bitcast.44, ...), custom_call_target="tpu_custom_call" | custom-call | tf_op jit(solution)/shard_map/block4/pallas_call | solution.py:401
  194.5 15.7 %all_to_all.58 = bf16[16,8,4096]{2,1,0:T(8,128)(2,1)S(1)} all-to-all(bf16[16,8,4096]{2,1,0:T(8,128)(2,1)S(1)} %bitcast.60), channel_id=1, replica_groups={{0,2,4,6,14,12,10,18,20,22,30,28,26,24,16,8},{1,3,5,7,15,13,11,19,21,23..., dimensions={0} | all-to-all | bytes 2097152 | tf_op jit(solution)/shard_map/all_to_all | solution.py:344
  210.2 0.1 convert_reduce_fusion
  210.4 4.4 %collective-permute-done.11.refs_3_ = bf16[8,4096]{1,0:T(8,128)(2,1)S(1)} collective-permute-done((bf16[8,4096]{1,0:T(8,128)(2,1)S(1)}, bf16[8,4096]{1,0:T(8,128)(2,1)S(1)}, u32[]{:S(2)}, u32[]{:S(2)}) %collective-permute-start.11) | collective-permute-done | bytes 65568 | tf_op jit(solution)/shard_map/ppermute | solution.py:411
  214.9 0.9 last_misfit.1
  215.8 10.1 %all-to-all-start.8 = ((f32[32,8,128]{2,1,0:T(8,128)}), f32[32,8,128]{2,1,0:T(8,128)S(1)}, u32[]{:S(2)}, u32[]{:S(2)}) async-start(f32[32,8,128]{2,1,0:T(8,128)} %bitcast.16), calls=%async_computation.8 | async-start | bytes 262144 | tf_op jit(solution)/shard_map/all_to_all | solution.py:422
  225.9 7.6 %all-to-all-done.8 = f32[32,8,128]{2,1,0:T(8,128)S(1)} async-done(((f32[32,8,128]{2,1,0:T(8,128)}), f32[32,8,128]{2,1,0:T(8,128)S(1)}, u32[]{:S(2)}, u32[]{:S(2)}) %all-to-all-start.8) | async-done | bytes 131104 | tf_op jit(solution)/shard_map/all_to_all | solution.py:422
  233.5 1.7 final.1
  235.3 0.6 copy.7
  (37 shorter events, 0.8 us)
Async XLA Ops:
  0.6 41.3 %collective-permute-start.2 = (bf16[344,4096]{1,0:T(8,128)(2,1)}, bf16[344,4096]{1,0:T(8,128)(2,1)S(1)}, u32[]{:S(2)}, u32[]{:S(2)}) collective-permute-start(bf16[344,4096]{1,0:T(8,128)(2,1)} %bitcast.20), channel_id=1, source_target_pairs={{0,1},{1,0},{2,3},{3,2},{4,5},{5,4},{6,7},{7,6},{8,9},{9,8},{10,11... | collective-permute-start | bytes 8454152 | tf_op jit(solution)/shard_map/ppermute | solution.py:354
  3.9 38.0 %collective-permute-start.3 = (bf16[344,4096]{1,0:T(8,128)(2,1)}, bf16[344,4096]{1,0:T(8,128)(2,1)S(1)}, u32[]{:S(2)}, u32[]{:S(2)}) collective-permute-start(bf16[344,4096]{1,0:T(8,128)(2,1)} %bitcast.29), channel_id=1, source_target_pairs={{0,1},{1,0},{2,3},{3,2},{4,5},{5,4},{6,7},{7,6},{8,9},{9,8},{10,11... | collective-permute-start | bytes 8454152 | tf_op jit(solution)/shard_map/ppermute | solution.py:354
  4.0 37.9 %collective-permute-start.4 = (bf16[344,4096]{1,0:T(8,128)(2,1)}, bf16[344,4096]{1,0:T(8,128)(2,1)S(1)}, u32[]{:S(2)}, u32[]{:S(2)}) collective-permute-start(bf16[344,4096]{1,0:T(8,128)(2,1)} %bitcast.45), channel_id=1, source_target_pairs={{0,1},{1,0},{2,3},{3,2},{4,5},{5,4},{6,7},{7,6},{8,9},{9,8},{10,11... | collective-permute-start | bytes 8454152 | tf_op jit(solution)/shard_map/ppermute | solution.py:354
  4.4 1.8 copy-start
  6.2 1.8 copy-start.2
  8.0 1.8 copy-start.4
  9.8 0.7 copy-start.7
  10.5 7.4 %copy-start.6 = (bf16[1,8,4096]{2,1,0:T(8,128)(2,1)S(1)}, bf16[1,8,4096]{2,1,0:T(8,128)(2,1)}, u32[]{:S(2)}) copy-start(bf16[1,8,4096]{2,1,0:T(8,128)(2,1)} %param.5) | copy-start | bytes 196612
  10.5 31.4 %copy-start.3 = (bf16[1,4096,344]{1,2,0:T(8,128)(2,1)S(1)}, bf16[1,4096,344]{1,2,0:T(8,128)(2,1)}, u32[]{:S(2)}) copy-start(bf16[1,4096,344]{1,2,0:T(8,128)(2,1)} %param.7) | copy-start | bytes 8454148
  12.7 29.3 %copy-start.1 = (bf16[1,4096,344]{1,2,0:T(8,128)(2,1)S(1)}, bf16[1,4096,344]{1,2,0:T(8,128)(2,1)}, u32[]{:S(2)}) copy-start(bf16[1,4096,344]{1,2,0:T(8,128)(2,1)} %param.6) | copy-start | bytes 8454148
  12.7 29.3 %copy-start.8 = (f32[1,4096]{1,0:T(1,128)S(1)}, f32[1,4096]{1,0:T(1,128)}, u32[]{:S(2)}) copy-start(f32[1,4096]{1,0:T(1,128)} %gain_ref.9) | copy-start | bytes 49156
  12.7 5.3 %collective-permute-start.1 = (bf16[8,512]{1,0:T(8,128)(2,1)S(1)}, bf16[8,512]{1,0:T(8,128)(2,1)S(1)}, u32[]{:S(2)}, u32[]{:S(2)}) collective-permute-start(bf16[8,512]{1,0:T(8,128)(2,1)S(1)} %start.1), channel_id=1, source_target_pairs={{0,33},{1,32},{2,35},{3,34},{4,37},{5,36},{6,39},{7,38},{8,41},{9,... | collective-permute-start | bytes 24584 | tf_op jit(solution)/shard_map/ppermute | solution.py:356
  12.8 5.2 %collective-permute-start = (bf16[8,512]{1,0:T(8,128)(2,1)S(1)}, bf16[8,512]{1,0:T(8,128)(2,1)S(1)}, u32[]{:S(2)}, u32[]{:S(2)}) collective-permute-start(bf16[8,512]{1,0:T(8,128)(2,1)S(1)} %start.1), channel_id=1, source_target_pairs={{0,32},{32,64},{64,96},{96,128},{128,160},{160,192},{192,224},{224... | collective-permute-start | bytes 24584 | tf_op jit(solution)/shard_map/ppermute | solution.py:355
  63.7 4.4 %collective-permute-start.5 = (bf16[8,4096]{1,0:T(8,128)(2,1)S(1)}, bf16[8,4096]{1,0:T(8,128)(2,1)S(1)}, u32[]{:S(2)}, u32[]{:S(2)}) collective-permute-start(bf16[8,4096]{1,0:T(8,128)(2,1)S(1)} %add_convert_fusion.3), channel_id=1, source_target_pairs={{0,32},{32,64},{64,96},{96,128},{128,160},{160,192},{192,224},{224... | collective-permute-start | bytes 196616 | tf_op jit(solution)/shard_map/ppermute | solution.py:411
  84.4 7.0 %copy-start.5 = (bf16[1,344,4096]{2,1,0:T(8,128)(2,1)S(1)}, bf16[1,344,4096]{2,1,0:T(8,128)(2,1)}, u32[]{:S(2)}) copy-start(bf16[1,344,4096]{2,1,0:T(8,128)(2,1)} %param.8) | copy-start | bytes 8454148
  87.6 3.8 %collective-permute-start.6 = (f32[8,128]{1,0:T(8,128)S(1)}, f32[8,128]{1,0:T(8,128)S(1)}, u32[]{:S(2)}, u32[]{:S(2)}) collective-permute-start(f32[8,128]{1,0:T(8,128)S(1)} %get-tuple-element.43.refs_0_), channel_id=1, source_target_pairs={{0,1},{1,0},{2,3},{3,2},{4,5},{5,4},{6,7},{7,6},{8,9},{9,8},{10,11... | collective-permute-start | bytes 12296 | tf_op jit(solution)/shard_map/ppermute | solution.py:394
  110.6 4.7 %collective-permute-start.7 = (bf16[8,4096]{1,0:T(8,128)(2,1)S(1)}, bf16[8,4096]{1,0:T(8,128)(2,1)S(1)}, u32[]{:S(2)}, u32[]{:S(2)}) collective-permute-start(bf16[8,4096]{1,0:T(8,128)(2,1)S(1)} %add_convert_fusion.2), channel_id=1, source_target_pairs={{0,32},{32,64},{64,96},{96,128},{128,160},{160,192},{192,224},{224... | collective-permute-start | bytes 196616 | tf_op jit(solution)/shard_map/ppermute | solution.py:411
  136.4 3.6 %collective-permute-start.8 = (f32[8,128]{1,0:T(8,128)S(1)}, f32[8,128]{1,0:T(8,128)S(1)}, u32[]{:S(2)}, u32[]{:S(2)}) collective-permute-start(f32[8,128]{1,0:T(8,128)S(1)} %get-tuple-element.52.refs_0_), channel_id=1, source_target_pairs={{0,1},{1,0},{2,3},{3,2},{4,5},{5,4},{6,7},{7,6},{8,9},{9,8},{10,11... | collective-permute-start | bytes 12296 | tf_op jit(solution)/shard_map/ppermute | solution.py:394
  160.0 4.5 %collective-permute-start.9 = (bf16[8,4096]{1,0:T(8,128)(2,1)S(1)}, bf16[8,4096]{1,0:T(8,128)(2,1)S(1)}, u32[]{:S(2)}, u32[]{:S(2)}) collective-permute-start(bf16[8,4096]{1,0:T(8,128)(2,1)S(1)} %add_convert_fusion.1), channel_id=1, source_target_pairs={{0,32},{32,64},{64,96},{96,128},{128,160},{160,192},{192,224},{224... | collective-permute-start | bytes 196616 | tf_op jit(solution)/shard_map/ppermute | solution.py:411
  186.8 3.0 %collective-permute-start.10 = (f32[8,128]{1,0:T(8,128)S(1)}, f32[8,128]{1,0:T(8,128)S(1)}, u32[]{:S(2)}, u32[]{:S(2)}) collective-permute-start(f32[8,128]{1,0:T(8,128)S(1)} %get-tuple-element.62.refs_0_), channel_id=1, source_target_pairs={{0,1},{1,0},{2,3},{3,2},{4,5},{5,4},{6,7},{7,6},{8,9},{9,8},{10,11... | collective-permute-start | bytes 12296 | tf_op jit(solution)/shard_map/ppermute | solution.py:394
  210.3 4.5 %collective-permute-start.11 = (bf16[8,4096]{1,0:T(8,128)(2,1)S(1)}, bf16[8,4096]{1,0:T(8,128)(2,1)S(1)}, u32[]{:S(2)}, u32[]{:S(2)}) collective-permute-start(bf16[8,4096]{1,0:T(8,128)(2,1)S(1)} %add_convert_fusion), channel_id=1, source_target_pairs={{0,32},{32,64},{64,96},{96,128},{128,160},{160,192},{192,224},{224... | collective-permute-start | bytes 196616 | tf_op jit(solution)/shard_map/ppermute | solution.py:411
  215.8 17.7 %all-to-all-start.8 = ((f32[32,8,128]{2,1,0:T(8,128)}), f32[32,8,128]{2,1,0:T(8,128)S(1)}, u32[]{:S(2)}, u32[]{:S(2)}) async-start(f32[32,8,128]{2,1,0:T(8,128)} %bitcast.16), calls=%async_computation.8 | async-start | bytes 262144 | tf_op jit(solution)/shard_map/all_to_all | solution.py:422
